TPU v7x, 32 devices: a whole 2x2x4 slice. The times are simulated.
32 devices in a mesh: seq: 16 (over z, x, core), chan: 2 (over y).
Axes of the slice: x: 2, y: 2, z: 4, core: 2. Of those that a mesh axis runs over, the one named last changes fastest.
Arguments:
- signal: bfloat16 [524288, 256], P('seq', 'chan'), parts along dimension 1, may hold values from -6 to 6
- gate_values: bfloat16 [524288, 256], P('seq', 'chan'), parts along dimension 1, may hold values from -4 to 4
- skip_gain: float32 [256], P('chan'), parts along dimension 0, may hold values from 0.25 to 2
- filter_spectrum: bfloat16 [2, 512, 1024, 256], P(None, 'seq', None, 'chan'), parts along dimension 3, may hold values from -4 to 4, as said below
Outputs:
- gated_output: bfloat16 [524288, 256], P('seq', 'chan'), parts along dimension 1
There are 2 independent parts, one for each index of `chan`. A program takes and returns all parts, laid end to end along the dimension named above; each array names one. Nothing has to cross between parts.
Inputs may be any that keep to these rules, and one draw needn't show every extreme that they name: `filter_spectrum`: the spectrum of a real filter: the complex entry at frequency k equals the conjugate of the entry at frequency (524288 - k) mod 524288.
All inputs are finite; a program needn't handle non-finite values.
Results may differ from a plain program's by a relative error of at most 0.0085.
Values may be sent and summed in bfloat16 or wider, within the bound.
A program may use at most 256 MiB of HBM per device.

v0:
```python
import functools
import math

import jax
import jax.numpy as jnp
from jax import lax
from jax.experimental import pallas as pl
from jax.experimental.pallas import tpu as pltpu
from jax.sharding import PartitionSpec as P

OUTER = 1024
INNER = 512
SEQ = 524288
MESH = pl.DeviceIdType.MESH


def tables(length):
    indices = lax.iota(jnp.int32, length)
    angles = (
        2.0 * math.pi / length * (indices[:, None] * indices[None, :] % length).astype(jnp.float32)
    )
    return (jnp.cos(angles).astype(jnp.bfloat16), jnp.sin(angles).astype(jnp.bfloat16))


def twiddle(c_values, b_values, length):
    angles = (
        2.0
        * math.pi
        / length
        * (c_values[:, None] * b_values[None, :] % length).astype(jnp.float32)
    )
    return (jnp.cos(angles), jnp.sin(angles))


def exchange(arrays, out_shape, moves, shards, collective_id):
    count = len(moves)

    def kernel(*refs):
        ins, out = refs[: len(arrays)], refs[len(arrays)]
        send_sem, recv_sem, own_sem = refs[len(arrays) + 1 :]
        me = lax.axis_index("seq")
        barrier = pltpu.get_barrier_semaphore()
        for i in range(1, shards):
            pl.semaphore_signal(
                barrier, inc=1, device_id={"seq": lax.rem(me + i, shards)}, device_id_type=MESH
            )
        pl.semaphore_wait(barrier, shards - 1)
        copies = []
        for i in range(1, shards):
            to = lax.rem(me + i, shards)
            for m, (which, take, put) in enumerate(moves):
                copies.append(
                    pltpu.make_async_remote_copy(
                        src_ref=ins[which].at[take(to)],
                        dst_ref=out.at[put(me)],
                        send_sem=send_sem.at[(i - 1) * count + m],
                        recv_sem=recv_sem.at[(i - 1) * count + m],
                        device_id={"seq": to},
                        device_id_type=MESH,
                    )
                )
                copies[-1].start()
        for m, (which, take, put) in enumerate(moves):
            copies.append(
                pltpu.make_async_copy(ins[which].at[take(me)], out.at[put(me)], own_sem.at[m])
            )
            copies[-1].start()
        for copy in copies:
            copy.wait()

    return pl.pallas_call(
        kernel,
        out_shape=jax.ShapeDtypeStruct(out_shape, jnp.bfloat16),
        in_specs=[pl.BlockSpec(memory_space=pl.ANY)] * len(arrays),
        out_specs=pl.BlockSpec(memory_space=pl.ANY),
        scratch_shapes=[
            pltpu.SemaphoreType.DMA(((shards - 1) * count,)),
            pltpu.SemaphoreType.DMA(((shards - 1) * count,)),
            pltpu.SemaphoreType.DMA((count,)),
        ],
        compiler_params=pltpu.CompilerParams(collective_id=collective_id, has_side_effects=True),
        name=f"exchange_{collective_id}",
    )(*arrays)


def block(index, size, base=0):
    return pl.ds(pl.multiple_of(base + index * size, math.gcd(base, size) if base else size), size)


def local(signal, gate_values, skip_gain, filter_spectrum):
    shards = lax.axis_size("seq")
    channels = signal.shape[1]
    ch_loc = channels // shards
    outer_loc = OUTER // shards
    inner_loc = INNER // shards
    rows = -(-(OUTER // 2 + 1) // 16) * 16
    cos_a, sin_a = tables(OUTER)
    cos_b, sin_b = tables(INNER)
    outer_scale = 1.0 / math.sqrt(OUTER)
    inner_scale = 1.0 / math.sqrt(INNER)
    fwd_b = jnp.concatenate(
        [jnp.concatenate([cos_b, sin_b], 1), jnp.concatenate([-sin_b, cos_b], 1)], 0
    )
    inv_b = jnp.concatenate(
        [jnp.concatenate([cos_b, -sin_b], 1), jnp.concatenate([sin_b, cos_b], 1)], 0
    )
    c_all = lax.iota(jnp.int32, rows)
    cos, sin = twiddle(lax.iota(jnp.int32, INNER), c_all, SEQ)
    every = slice(None)

    def lead(size):
        return lambda t: (block(t, size), every, every)

    def middle(size):
        return lambda t: (every, block(t, size), every)

    grid = exchange(
        [signal.T.reshape(channels, outer_loc, INNER)],
        (ch_loc, OUTER, INNER),
        [(0, lead(ch_loc), middle(outer_loc))],
        shards,
        0,
    )
    filt = [
        exchange(
            [filter_spectrum[p, :, :rows].transpose(2, 0, 1)],
            (ch_loc, INNER, rows),
            [(0, lead(ch_loc), middle(inner_loc))],
            shards,
            1 + p,
        ).astype(jnp.float32)
        for p in range(2)
    ]
    fwd_re = jnp.einsum(
        "kab,ac->kbc", grid, cos_a[:, :rows], preferred_element_type=jnp.float32
    )
    fwd_im = -jnp.einsum(
        "kab,ac->kbc", grid, sin_a[:, :rows], preferred_element_type=jnp.float32
    )
    q = jnp.concatenate(
        [
            (fwd_re * cos + fwd_im * sin) * outer_scale,
            (fwd_im * cos - fwd_re * sin) * outer_scale,
        ],
        axis=1,
    ).astype(jnp.bfloat16)
    spectrum = jnp.einsum("db,kbc->kdc", fwd_b, q, preferred_element_type=jnp.float32)
    spectrum = (spectrum * inner_scale).astype(jnp.bfloat16).astype(jnp.float32)
    re, im = spectrum[:, :INNER], spectrum[:, INNER:]
    product = jnp.concatenate(
        [re * filt[0] - im * filt[1], re * filt[1] + im * filt[0]], axis=1
    ).astype(jnp.bfloat16)
    back = jnp.einsum("bd,kdc->kbc", inv_b, product, preferred_element_type=jnp.float32)
    back = back * inner_scale
    re, im = back[:, :INNER], back[:, INNER:]
    r_re = (re * cos - im * sin).astype(jnp.bfloat16)
    r_im = (re * sin + im * cos).astype(jnp.bfloat16)
    weight = jnp.where((c_all == 0) | (c_all == OUTER // 2), 1.0, 2.0)
    weight = jnp.where(c_all > OUTER // 2, 0.0, weight).astype(jnp.bfloat16)[None, :]
    convolved = (
        jnp.einsum(
            "ac,kbc->kab", cos_a[:, :rows] * weight, r_re, preferred_element_type=jnp.float32
        )
        - jnp.einsum(
            "ac,kbc->kab", sin_a[:, :rows] * weight, r_im, preferred_element_type=jnp.float32
        )
    ) * outer_scale
    convolved = exchange(
        [convolved.astype(jnp.bfloat16)],
        (channels, outer_loc, INNER),
        [(0, middle(outer_loc), lead(ch_loc))],
        shards,
        3,
    )
    convolved = convolved.reshape(channels, outer_loc * INNER).T
    result = gate_values.astype(jnp.float32) * (
        convolved.astype(jnp.float32) + skip_gain[None, :] * signal.astype(jnp.float32)
    )
    return result.astype(jnp.bfloat16)


def solution(mesh):
    return jax.shard_map(
        local,
        mesh=mesh,
        in_specs=(P("seq", "chan"), P("seq", "chan"), P("chan"), P(None, "seq", None, "chan")),
        out_specs=P("seq", "chan"),
        check_vma=False,
    )
```

profile of v0, /device:TPU:11, one launch (start us, length us, event | category | flops | bytes accessed | tf_op | source)
XLA Modules:
  0.0 890.5 jit_solution(4025072793836846918)
XLA Ops:
  4.0 12.8 %copy.40.refs_0_ = bf16[128,64,512]{2,1,0:T(8,128)(2,1)} copy(bf16[128,64,512]{0,2,1:T(8,128)(2,1)} %bitcast.66) | data formatting | bytes 16777216 | tf_op jit(solution)/shard_map/reshape | solution.py:118
  16.8 185.6 %exchange_0.1 = bf16[8,1024,512]{2,1,0:T(8,128)(2,1)} custom-call(bf16[128,64,512]{2,1,0:T(8,128)(2,1)} %copy.40.refs_0_), custom_call_target="tpu_custom_call" | custom-call | tf_op jit(solution)/shard_map/exchange_0/pallas_call | solution.py:71
  202.4 15.2 %fusion.41 = f32[528,8,512]{2,0,1:T(8,128)S(1)} fusion(bf16[8,1024,512]{2,1,0:T(8,128)(2,1)} %exchange_0.1, f32[1024,1024]{0,1:T(8,128)} %fusion.22), kind=kOutput, calls=%fused_computation.70 | convolution fusion | flops 4429725696 | bytes 19202048 | tf_op jit(solution)/shard_map/kab,ac->kbc/dot_general | solution.py:137
  217.6 11.2 %fusion.43 = f32[528,8,512]{2,0,1:T(8,128)S(1)} fusion(bf16[8,1024,512]{2,1,0:T(8,128)(2,1)S(1)} %copy-done, f32[1024,1024]{0,1:T(8,128)S(1)} %copy-done.1), kind=kOutput, calls=%fused_computation.72 | convolution fusion | flops 4429725696 | bytes 19202048 | tf_op jit(solution)/shard_map/kab,ac->kbc/dot_general | solution.py:134
  228.8 4.2 fusion.58
  233.0 18.3 %fusion.8 = (bf16[8,512,528]{1,0,2:T(8,128)(2,1)}, bf16[8,512,528]{1,0,2:T(8,128)(2,1)}) fusion(f32[528,8,512]{2,0,1:T(8,128)S(1)} %fusion.43, f32[528,8,512]{2,0,1:T(8,128)S(1)} %fusion.41, f32[512,528]{0,1:T(8,128)S(1)} %get-tuple-element.13, f32[512,528]{0,1:T(8,128)S(1)} %get-tuple-element.14), kind=kLoop, calls=%fused_computation.21 | loop fusion | flops 23789568 | bytes 28114944 | tf_op jit(solution)/shard_map/convert.5
  251.3 8.1 pad_maximum_fusion.1
  259.4 4.3 sine_convert_fusion.1
  267.7 54.2 %convert_bitcast_fusion = f32[8,1024,528]{2,1,0:T(8,128)} fusion(bf16[8,1024,528]{1,0,2:T(8,128)(2,1)} %pad_maximum_fusion.1, bf16[512,512]{1,0:T(8,128)(2,1)S(1)} %get-tuple-element.16, bf16[512,512]{1,0:T(8,128)(2,1)S(1)} %fusion.60, bf16[512,512]{1,0:T(8,128)(2,1)S(1)} %get-tuple-element.15), kind=kOutput, calls=%fused_computation | convolution fusion | flops 8879734784 | bytes 27525120 | tf_op jit(solution)/shard_map/db,kbc->kdc/dot_general | solution.py:147
  322.0 6.2 fusion.64
  328.1 8.9 copy.43
  337.0 117.1 %exchange_1.1 = bf16[8,512,528]{2,1,0:T(8,128)(2,1)} custom-call(bf16[128,32,528]{2,1,0:T(8,128)(2,1)} %bitcast.67), custom_call_target="tpu_custom_call" | custom-call | tf_op jit(solution)/shard_map/exchange_1/pallas_call | solution.py:71
  454.1 8.9 copy.44
  463.0 117.2 %exchange_2.1 = bf16[8,512,528]{2,1,0:T(8,128)(2,1)} custom-call(bf16[128,32,528]{2,1,0:T(8,128)(2,1)} %bitcast.68), custom_call_target="tpu_custom_call" | custom-call | tf_op jit(solution)/shard_map/exchange_2/pallas_call | solution.py:71
  580.2 11.7 %fusion.3 = (bf16[8,512,528]{2,1,0:T(8,128)(2,1)S(1)}, bf16[8,512,528]{2,1,0:T(8,128)(2,1)S(1)}) fusion(bf16[8,512,528]{2,1,0:T(8,128)(2,1)} %exchange_1.1, bf16[8,512,528]{2,1,0:T(8,128)(2,1)} %exchange_2.1, f32[8,1024,528]{2,1,0:T(8,128)} %convert_bitcast_fusion), kind=kLoop, calls=%fused_computation.12 | loop fusion | flops 21626880 | bytes 34603008 | tf_op jit(solution)/shard_map/convert.3
  591.9 5.7 pad_maximum_fusion
  597.6 15.2 %copy.36 = bf16[8,1024,528]{1,0,2:T(8,128)(2,1)} copy(bf16[8,1024,528]{2,1,0:T(8,128)(2,1)} %pad_maximum_fusion) | data formatting | bytes 17301504 | tf_op jit(solution)/shard_map/concatenate | solution.py:150
  612.8 15.0 %multiply_bitcast_fusion = f32[8,1024,528]{1,0,2:T(8,128)} fusion(bf16[8,1024,528]{1,0,2:T(8,128)(2,1)} %copy.36, bf16[512,512]{1,0:T(8,128)(2,1)S(1)} %get-tuple-element.16, bf16[512,512]{1,0:T(8,128)(2,1)S(1)} %get-tuple-element.15, bf16[512,512]{1,0:T(8,128)(2,1)} %copy-done.4), kind=kOutput, calls=%fused_computation.2 | convolution fusion | flops 8871084032 | bytes 27525120 | tf_op jit(solution)/shard_map/bd,kdc->kbc/dot_general | solution.py:153
  627.8 8.1 add_convert_fusion
  635.9 18.6 %fusion.18 = f32[8,512,1024]{1,2,0:T(8,128)} fusion(bf16[8,512,528]{1,0,2:T(8,128)(2,1)S(1)} %get-tuple-element.8, bf16[528]{0:T(1024)(128)(2,1)S(1)} %select_convert_fusion, f32[1024,1024]{0,1:T(8,128)S(1)} %copy-done.2), kind=kOutput, calls=%fused_computation.37 | convolution fusion | flops 4431888384 | bytes 23267328 | tf_op jit(solution)/shard_map/ac,kbc->kab/dot_general | solution.py:161
  654.5 21.1 %fusion.16.refs_0_ = bf16[8,1024,512]{2,1,0:T(8,128)(2,1)} fusion(f32[8,512,1024]{1,2,0:T(8,128)} %fusion.18, bf16[8,512,528]{1,0,2:T(8,128)(2,1)S(1)} %get-tuple-element.7, bf16[528]{0:T(1024)(128)(2,1)S(1)} %select_convert_fusion, f32[1024,1024]{0,1:T(8,128)S(1)} %copy-done.3), kind=kOutput, calls=%fused_computation.35 | convolution fusion | flops 4444471296 | bytes 31655936 | tf_op jit(solution)/shard_map/ac,kbc->kab/dot_general | solution.py:164
  675.6 184.6 %exchange_3.1 = bf16[128,64,512]{2,1,0:T(8,128)(2,1)} custom-call(bf16[8,1024,512]{2,1,0:T(8,128)(2,1)} %fusion.16.refs_0_), custom_call_target="tpu_custom_call" | custom-call | tf_op jit(solution)/shard_map/exchange_3/pallas_call | solution.py:71
  860.2 14.7 %copy.42 = f32[128,64,512]{0,2,1:T(8,128)} copy(bf16[128,64,512]{2,1,0:T(8,128)(2,1)} %exchange_3.1) | data formatting | bytes 25165824 | tf_op jit(solution)/shard_map/convert_element_type | solution.py:177
  874.8 15.2 %fusion.1 = bf16[32768,128]{1,0:T(8,128)(2,1)} fusion(f32[128,64,512]{0,2,1:T(8,128)} %copy.42, bf16[32768,128]{1,0:T(8,128)(2,1)} %param.4, bf16[32768,128]{1,0:T(8,128)(2,1)} %param.5, f32[128]{0:T(128)S(1)} %copy-done.5), kind=kLoop, calls=%fused_computation.5 | loop fusion | flops 25165824 | bytes 41943552 | tf_op jit(solution)/shard_map/convert_element_type | solution.py:179
  (15 shorter events, 8.0 us)
Async XLA Ops:
  202.4 15.2 %copy-start = (bf16[8,1024,512]{2,1,0:T(8,128)(2,1)S(1)}, bf16[8,1024,512]{2,1,0:T(8,128)(2,1)}, u32[]{:S(2)}) copy-start(bf16[8,1024,512]{2,1,0:T(8,128)(2,1)} %exchange_0.1) | copy-start | bytes 25165828
  202.4 15.2 %copy-start.1 = (f32[1024,1024]{0,1:T(8,128)S(1)}, f32[1024,1024]{0,1:T(8,128)}, u32[]{:S(2)}) copy-start(f32[1024,1024]{0,1:T(8,128)} %fusion.22) | copy-start | bytes 12582916
  267.7 54.2 %copy-start.4 = (bf16[512,512]{1,0:T(8,128)(2,1)}, bf16[512,512]{1,0:T(8,128)(2,1)S(1)}, u32[]{:S(2)}) copy-start(bf16[512,512]{1,0:T(8,128)(2,1)S(1)} %fusion.60) | copy-start | bytes 1572868
  627.8 8.1 copy-start.2
  635.9 18.6 %copy-start.3 = (f32[1024,1024]{0,1:T(8,128)S(1)}, f32[1024,1024]{0,1:T(8,128)}, u32[]{:S(2)}) copy-start(f32[1024,1024]{0,1:T(8,128)} %fusion.22) | copy-start | bytes 12582916
  860.2 14.7 %copy-start.5 = (f32[128]{0:T(128)S(1)}, f32[128]{0:T(128)}, u32[]{:S(2)}) copy-start(f32[128]{0:T(128)} %param.6) | copy-start | bytes 1540
where the time goes:
time: 894 us; the launch traced here: 891 us
  Pallas kernels  604 us (68%)
  matrix products  135 us (15%)
  other arithmetic  83.6 us (9%)
  local copies, waits for them, and re-layouts  66.6 us (7%)
    pallas_call x4, Pallas kernels, exchange(): pl.pallas_call(kernel, out_shape=jax.ShapeDtypeStruct(out_shape, jnp.bflo...  604 us
    dot_general x1, matrix products, local(): jnp.einsum('db,kbc->kdc', fwd_b, q, preferred_element_type=jnp.float32)  54.2 us
    another operation x2, other arithmetic  30 us
    dot_general x1, matrix products, local(): jnp.einsum('ac,kbc->kab', sin_a[:, :rows] * weight, r_im, preferred_eleme...  21.1 us
    dot_general x1, matrix products, local(): jnp.einsum('ac,kbc->kab', cos_a[:, :rows] * weight, r_re, preferred_eleme...  18.6 us

commit v1 on v0

v1 whole, which is shorter than its diff:
```python
import math

import jax
import jax.numpy as jnp
from jax import lax
from jax.experimental import pallas as pl
from jax.experimental.pallas import tpu as pltpu
from jax.sharding import PartitionSpec as P

MESH = pl.DeviceIdType.MESH


def tables(length, rows=None, columns=None):
    rows = lax.iota(jnp.int32, length) if rows is None else rows
    columns = lax.iota(jnp.int32, length) if columns is None else columns
    angles = 2.0 * math.pi / length * (rows[:, None] * columns[None, :] % length).astype(jnp.float32)
    return (jnp.cos(angles).astype(jnp.bfloat16), jnp.sin(angles).astype(jnp.bfloat16))


def twiddle(c_values, b_values, length):
    angles = (
        2.0
        * math.pi
        / length
        * (c_values[:, None] * b_values[None, :] % length).astype(jnp.float32)
    )
    return (jnp.cos(angles), jnp.sin(angles))


def flip(me, i, shards):
    out, bit = 0, 1
    while bit < shards:
        out = out + lax.rem(lax.div(me, bit) + lax.div(i, bit), 2) * bit
        bit *= 2
    return out


def matmul(a, b):
    return lax.dot_general(a, b, (((1,), (0,)), ((), ())), preferred_element_type=jnp.float32)


def matmul_nt(a, b):
    return lax.dot_general(a, b, (((1,), (1,)), ((), ())), preferred_element_type=jnp.float32)


def convolve(sig, filt, ext, outer, fwd, inv, tw_cb, tw_bc, shards):
    ch_loc, a_loc, inner = sig.shape[1:]
    d_loc, n_outer = filt.shape[3:]
    half = shards // 2
    d_half = half * d_loc
    step = 256
    chunks = n_outer // step
    inner_scale = 1.0 / math.sqrt(inner)
    ahead = min(3, ch_loc)
    last = pl.ds(0, shards - 1)

    def kernel(
        sig_ref, filt_ref, ext_ref, outer_ref, fwd_ref, inv_ref, tcb_ref, tbc_ref, conv_ref,
        s_buf, f_buf, e_buf, outer_t, fwd_t, inv_t, tcb, tbc, r_buf, o_buf,
        sig_send, sig_recv, filt_send, filt_recv, ext_send, ext_recv,
        out_send, out_recv, table_sem,
    ):
        me = lax.axis_index("seq")
        side = lax.div(me, half)
        mine = lax.rem(me, half)
        barrier = pltpu.get_barrier_semaphore()

        def greet(i, carry):
            pl.semaphore_signal(
                barrier, inc=1, device_id={"seq": lax.rem(me + i, shards)}, device_id_type=MESH
            )
            return carry

        lax.fori_loop(1, shards, greet, 0)
        pl.semaphore_wait(barrier, shards - 1)

        def rows(s):
            return pl.ds(pl.multiple_of(s * a_loc, a_loc), a_loc)

        def send_round(k):
            def send_signal(i, carry):
                to = flip(me, shards - i, shards)
                pltpu.make_async_remote_copy(
                    src_ref=sig_ref.at[to, k],
                    dst_ref=s_buf.at[k, rows(me)],
                    send_sem=sig_send.at[k],
                    recv_sem=sig_recv.at[k],
                    device_id={"seq": to},
                    device_id_type=MESH,
                ).start()
                return carry

            def send_filter(i, carry):
                to = flip(me, half - i, shards)
                pltpu.make_async_remote_copy(
                    src_ref=filt_ref.at[to, k],
                    dst_ref=f_buf.at[k, :, mine],
                    send_sem=filt_send.at[k],
                    recv_sem=filt_recv.at[k],
                    device_id={"seq": to},
                    device_id_type=MESH,
                ).start()
                return carry

            lax.fori_loop(1, shards, send_signal, 0)
            lax.fori_loop(1, half, send_filter, 0)
            pltpu.make_async_copy(sig_ref.at[me, k], s_buf.at[k, rows(me)], sig_recv.at[k]).start()
            pltpu.make_async_copy(filt_ref.at[me, k], f_buf.at[k, :, mine], filt_recv.at[k]).start()

        @pl.when(mine == 0)
        def _():
            def send_ext(i, carry):
                to = (1 - side) * half + i
                pltpu.make_async_remote_copy(
                    src_ref=ext_ref.at[to],
                    dst_ref=e_buf,
                    send_sem=ext_send,
                    recv_sem=ext_recv,
                    device_id={"seq": to},
                    device_id_type=MESH,
                ).start()
                return carry

            lax.fori_loop(0, half, send_ext, 0)

        for k in range(ahead):
            send_round(k)
        loads = [
            pltpu.make_async_copy(src, dst, table_sem.at[i])
            for i, (src, dst) in enumerate(
                [
                    (outer_ref, outer_t),
                    (fwd_ref, fwd_t),
                    (inv_ref, inv_t),
                    (tcb_ref, tcb),
                    (tbc_ref, tbc),
                ]
            )
        ]
        for load in loads:
            load.start()
        for load in loads:
            load.wait()
        pltpu.make_async_copy(e_buf, e_buf, ext_recv).wait()

        b_row = lax.broadcasted_iota(jnp.int32, (1, inner), 1)
        b_col = lax.broadcasted_iota(jnp.int32, (inner, 1), 0)
        swing = (1 - side).astype(jnp.float32)
        sign_row = 1.0 - 2.0 * swing * (b_row % 2).astype(jnp.float32)
        sign_col = 1.0 - 2.0 * swing * (b_col % 2).astype(jnp.float32)

        def channel(k, carry):
            slot = lax.rem(k, 2)

            @pl.when(k + ahead < ch_loc)
            def _():
                send_round(k + ahead)

            pltpu.make_async_copy(s_buf.at[k], s_buf.at[k], sig_recv.at[k]).wait()
            pltpu.make_async_copy(f_buf.at[k], f_buf.at[k], filt_recv.at[k]).wait()
            special = e_buf[k, :, 0:1]

            def forward(j, carry):
                at = pl.multiple_of(j * step, step)
                here = pl.ds(at, step)
                x = s_buf[k]
                f_re = matmul(outer_t[here, :], x)
                f_im = matmul(outer_t[pl.ds(pl.multiple_of(n_outer + at, step), step), :], x)
                cos, sin = tcb[0, here, :], tcb[1, here, :]
                q_re = (f_re * cos + f_im * sin).astype(jnp.bfloat16)
                q_im = (f_im * cos - f_re * sin).astype(jnp.bfloat16)
                q = jnp.concatenate([q_re, q_im], axis=1)
                spectrum = matmul_nt(fwd_t[...], q) * inner_scale
                spectrum = spectrum.astype(jnp.bfloat16).astype(jnp.float32)
                s_re, s_im = spectrum[:d_half], spectrum[d_half:]
                h_re = f_buf[k, 0, :, :, here].astype(jnp.float32).reshape(d_half, step)
                h_im = f_buf[k, 1, :, :, here].astype(jnp.float32).reshape(d_half, step)
                d_at = lax.broadcasted_iota(jnp.int32, (d_half, step), 0)
                c_at = lax.broadcasted_iota(jnp.int32, (d_half, step), 1) + at
                share = jnp.where((d_at == 0) & (c_at == 0), 0.5, 1.0)
                product = jnp.concatenate(
                    [(s_re * h_re - s_im * h_im) * share, (s_re * h_im + s_im * h_re) * share],
                    axis=0,
                ).astype(jnp.bfloat16)
                edge = jnp.sum(q_re[0:1].astype(jnp.float32) * sign_row, axis=1, keepdims=True)
                edge = (edge * inner_scale).astype(jnp.bfloat16).astype(jnp.float32)
                edge = (edge * special).astype(jnp.bfloat16).astype(jnp.float32) * 0.5
                c_row = lax.broadcasted_iota(jnp.int32, (1, step), 1) + at
                edge = jnp.where(c_row == 0, edge, 0.0)
                u = matmul(inv_t[...], product)
                u_re, u_im = u[:inner] + sign_col * edge, u[inner:]
                cos, sin = tbc[0, :, here], tbc[1, :, here]
                r_buf[0, :, here] = (u_re * cos - u_im * sin).astype(jnp.bfloat16)
                r_buf[1, :, here] = (u_re * sin + u_im * cos).astype(jnp.bfloat16)
                return carry

            lax.fori_loop(0, chunks, forward, 0)

            @pl.when(k >= 2)
            def _():
                pltpu.make_async_copy(o_buf.at[slot], o_buf.at[slot], out_send.at[slot]).wait()

            def backward(j, carry):
                at = pl.multiple_of(j * step, step)
                conv = matmul_nt(outer_t[pl.ds(at, step), :], r_buf[0]) + matmul_nt(
                    outer_t[pl.ds(pl.multiple_of(n_outer + at, step), step), :], r_buf[1]
                )
                conv = conv * (2.0 / math.sqrt(n_outer))
                o_buf[slot, pl.ds(at, step), :] = conv.astype(jnp.bfloat16)
                return carry

            lax.fori_loop(0, chunks, backward, 0)
            pltpu.make_async_copy(
                o_buf.at[slot, rows(me)], conv_ref.at[me, k], out_send.at[slot]
            ).start()

            def send_out(i, carry):
                to = flip(me, shards - i, shards)
                pltpu.make_async_remote_copy(
                    src_ref=o_buf.at[slot, rows(to)],
                    dst_ref=conv_ref.at[me, k],
                    send_sem=out_send.at[slot],
                    recv_sem=out_recv,
                    device_id={"seq": to},
                    device_id_type=MESH,
                ).start()
                return carry

            lax.fori_loop(1, shards, send_out, 0)
            return carry

        lax.fori_loop(0, ch_loc, channel, 0)
        for slot in range(min(2, ch_loc)):
            pltpu.make_async_copy(o_buf.at[slot], o_buf.at[slot], out_send.at[slot]).wait()
        for k in range(ch_loc):
            pltpu.make_async_copy(sig_ref.at[last, k], sig_ref.at[last, k], sig_send.at[k]).wait()
            own = filt_ref.at[pl.ds(0, half - 1), k]
            pltpu.make_async_copy(own, own, filt_send.at[k]).wait()

        @pl.when(mine == 0)
        def _():
            own = ext_ref.at[pl.ds(0, half)]
            pltpu.make_async_copy(own, own, ext_send).wait()

        pltpu.make_async_copy(conv_ref.at[last], conv_ref.at[last], out_recv).wait()

    anywhere = pl.BlockSpec(memory_space=pl.ANY)
    bf16 = jnp.bfloat16
    return pl.pallas_call(
        kernel,
        out_shape=jax.ShapeDtypeStruct(sig.shape, bf16),
        in_specs=[anywhere] * 8,
        out_specs=anywhere,
        scratch_shapes=[
            pltpu.VMEM((ch_loc, shards * a_loc, inner), bf16),
            pltpu.VMEM((ch_loc, 2, half, d_loc, n_outer), bf16),
            pltpu.VMEM(ext.shape[1:], jnp.float32),
            pltpu.VMEM(outer.shape, bf16),
            pltpu.VMEM(fwd.shape, bf16),
            pltpu.VMEM(inv.shape, bf16),
            pltpu.VMEM(tw_cb.shape, jnp.float32),
            pltpu.VMEM(tw_bc.shape, jnp.float32),
            pltpu.VMEM((2, inner, n_outer), bf16),
            pltpu.VMEM((2, n_outer, inner), bf16),
            pltpu.SemaphoreType.DMA((ch_loc,)),
            pltpu.SemaphoreType.DMA((ch_loc,)),
            pltpu.SemaphoreType.DMA((ch_loc,)),
            pltpu.SemaphoreType.DMA((ch_loc,)),
            pltpu.SemaphoreType.DMA,
            pltpu.SemaphoreType.DMA,
            pltpu.SemaphoreType.DMA((2,)),
            pltpu.SemaphoreType.DMA,
            pltpu.SemaphoreType.DMA((5,)),
        ],
        compiler_params=pltpu.CompilerParams(
            collective_id=0, has_side_effects=True, vmem_limit_bytes=63 * 1024 * 1024
        ),
        name="convolve",
    )(sig, filt, ext, outer, fwd, inv, tw_cb, tw_bc)


def local(signal, gate_values, skip_gain, filter_spectrum):
    shards = lax.axis_size("seq")
    me = lax.axis_index("seq")
    positions, channels = signal.shape
    d_loc, n_outer = filter_spectrum.shape[1:3]
    inner = d_loc * shards
    length = n_outer * inner
    ch_loc = channels // shards
    a_loc = n_outer // shards
    half = shards // 2
    side = me // half
    outer_scale = 1.0 / math.sqrt(n_outer)
    inner_scale = 1.0 / math.sqrt(inner)

    cos_a, sin_a = tables(n_outer)
    outer = jnp.concatenate([cos_a, -sin_a], 0)
    d_values = side * (inner // 2) + lax.iota(jnp.int32, inner // 2)
    cos_b, sin_b = tables(inner, d_values)
    fwd = jnp.concatenate(
        [jnp.concatenate([cos_b, sin_b], 1), jnp.concatenate([-sin_b, cos_b], 1)], 0
    )
    inv = fwd.T
    cos, sin = twiddle(lax.iota(jnp.int32, n_outer), lax.iota(jnp.int32, inner), length)
    tw_cb = jnp.stack([cos, sin]) * outer_scale
    tw_bc = jnp.stack([cos.T, sin.T]) * inner_scale

    sig = signal.T.reshape(shards, ch_loc, a_loc, inner)
    filt = filter_spectrum.transpose(3, 0, 1, 2).reshape(shards, ch_loc, 2, d_loc, n_outer)
    ext = jnp.broadcast_to(
        filter_spectrum[0, 0, 0].astype(jnp.float32).reshape(shards, ch_loc, 1, 1),
        (shards, ch_loc, 1, 128),
    )
    convolved = convolve(sig, filt, ext, outer, fwd, inv, tw_cb, tw_bc, shards)
    convolved = convolved.reshape(channels, positions).T
    result = gate_values.astype(jnp.float32) * (
        convolved.astype(jnp.float32) + skip_gain[None, :] * signal.astype(jnp.float32)
    )
    return result.astype(jnp.bfloat16)


def solution(mesh):
    return jax.shard_map(
        local,
        mesh=mesh,
        in_specs=(P("seq", "chan"), P("seq", "chan"), P("chan"), P(None, "seq", None, "chan")),
        out_specs=P("seq", "chan"),
        check_vma=False,
    )
```

time: 894 us -> 555 us (0.62)
  Pallas kernels: 604 us -> 378 us
  matrix products: 135 us -> 0 us
  local copies, waits for them, and re-layouts: 66.6 us -> 82.9 us
    pallas_call x4 -> x1, Pallas kernels: 604 us -> 378 us  [convolve(): pl.pallas_call(kernel, out_shape=jax.ShapeDtypeStruct(sig.shape, bf16), i...]
    dot_general x6 -> x0, matrix products: 135 us -> none  [the longest x1 54.2 us: local(): jnp.einsum('db,kbc->kdc', fwd_b, q, preferred_element_type=jnp.float32)]
    transpose x0 -> x2, local copies, waits for them, and re-layouts: none -> 35.4 us  [the longest x1 23.5 us: local(): filter_spectrum.transpose(3, 0, 1, 2)]
    another operation x2 -> x0, other arithmetic: 30 us -> none
    neg x0 -> x1, other arithmetic: none -> 15.8 us  [local(): outer = jnp.concatenate([cos_a, -sin_a], 0)]
    concatenate x1, local copies, waits for them, and re-layouts: 15.2 us -> 1.31 us  [local(): jnp.concatenate([jnp.concatenate([cos_b, sin_b], 1), jnp.concatenate([-si...]
    reshape x1 -> x0, local copies, waits for them, and re-layouts: 12.8 us -> none  [local(): signal.T.reshape(channels, outer_loc, INNER)]
    sin x1 -> x2, other arithmetic: 4.22 us -> 16.5 us  [twiddle(): return (jnp.cos(angles), jnp.sin(angles))]
where the time goes in v1:
time: 555 us; the launch traced here: 550 us
  Pallas kernels  378 us (68%)
  other arithmetic  88.4 us (16%)
  local copies, waits for them, and re-layouts  82.9 us (15%)
    pallas_call x1, Pallas kernels, convolve(): pl.pallas_call(kernel, out_shape=jax.ShapeDtypeStruct(sig.shape, bf16), i...  378 us
    unnamed x4, local copies, waits for them, and re-layouts  27.8 us
    transpose x1, local copies, waits for them, and re-layouts, local(): filter_spectrum.transpose(3, 0, 1, 2)  23.5 us
    convert_element_type x1, local copies, waits for them, and re-layouts, local(): convolved.astype(jnp.float32)  17.4 us
    sin x2, other arithmetic, twiddle(): return (jnp.cos(angles), jnp.sin(angles))  16.5 us
    neg x1, other arithmetic, local(): outer = jnp.concatenate([cos_a, -sin_a], 0)  15.8 us
    convert_element_type x1, other arithmetic, tables(): jnp.cos(angles).astype(jnp.bfloat16)  15.7 us
    convert_element_type x1, other arithmetic, local(): return result.astype(jnp.bfloat16)  15.2 us

profile of v1, /device:TPU:11, one launch (start us, length us, event | category | flops | bytes accessed | tf_op | source)
XLA Modules:
  0.0 549.7 jit_solution(7665761519146196723)
XLA Ops:
  0.0 0.7 convert_reduce_fusion
  0.7 0.1 reshape.162
  0.8 0.8 broadcast_in_dim.2.ext_ref
  1.6 2.0 fusion.31
  3.6 2.2 sine_convert_fusion.1
  5.9 1.1 fusion.32
  7.0 1.3 copy.11.fwd_ref
  8.3 15.8 %fusion.14 = bf16[1024,1024]{1,0:T(8,128)(2,1)S(1)} fusion(), kind=kLoop, calls=%fused_computation.31 | loop fusion | flops 18874368 | bytes 2097152 | tf_op jit(solution)/shard_map/neg | solution.py:297
  24.1 15.7 %cosine_convert_fusion = bf16[1024,1024]{1,0:T(8,128)(2,1)S(1)} fusion(), kind=kLoop, calls=%fused_computation.15 | loop fusion | flops 15728640 | bytes 2097152 | tf_op jit(solution)/shard_map/convert_element_type | solution.py:17
  39.9 2.5 pad_maximum_fusion.outer_ref
  42.3 8.2 %fusion.23 = (f32[1,1024,512]{2,1,0:T(8,128)S(1)}, f32[1,1024,512]{2,1,0:T(8,128)S(1)}) fusion(), kind=kLoop, calls=%fused_computation.41 | loop fusion | flops 7340032 | bytes 4194304 | tf_op jit(solution)/shard_map/sin | solution.py:27
  50.5 2.6 maximum_multiply_fusion.tcb_ref
  53.1 8.4 %fusion.21 = (f32[1,512,1024]{2,1,0:T(8,128)S(1)}, f32[1,512,1024]{2,1,0:T(8,128)S(1)}) fusion(), kind=kLoop, calls=%fused_computation.39 | loop fusion | flops 7340032 | bytes 4194304 | tf_op jit(solution)/shard_map/sin | solution.py:27
  61.5 2.4 maximum_multiply_fusion.1.tbc_ref
  63.9 11.9 %copy.9 = bf16[128,32768]{1,0:T(8,128)(2,1)} copy(bf16[128,32768]{0,1:T(8,128)(2,1)} %bitcast.23) | data formatting | bytes 16777216 | tf_op jit(solution)/shard_map/transpose | solution.py:308
  75.8 10.1 %copy.16 = bf16[16,8,64,512]{3,2,1,0:T(8,128)(2,1)} copy(bf16[16,8,64,512]{3,1,2,0:T(8,128)(2,1)} %bitcast.22) | data formatting | bytes 16777216
  85.9 23.5 %copy.10 = bf16[128,2,32,1024]{3,2,1,0:T(8,128)(2,1)} copy(bf16[128,2,32,1024]{0,3,2,1:T(8,128)(2,1)} %bitcast.24) | data formatting | bytes 33554432 | tf_op jit(solution)/shard_map/transpose | solution.py:309
  109.4 378.3 %convolve.1 = bf16[16,8,64,512]{3,2,1,0:T(8,128)(2,1)} custom-call(bf16[16,8,64,512]{3,2,1,0:T(8,128)(2,1)} %copy.16, bf16[16,8,2,32,1024]{4,3,2,1,0:T(8,128)(2,1)} %bitcast.20, f32[16,8,1,128]{3,2,1,0:T(1,128)} %broadcast_in_dim.2.ext_ref, bf16[2048,1024]{1,0:T(8,128)(2,1)} %pad_maximum_fusion.outer_ref, bf16[512,1024]{1,0:T(8,128)(2,1)} %copy.11.fwd_ref, ...), custom_call_target="tpu_custom_call" | custom-call | tf_op jit(solution)/shard_map/convolve/pallas_call | solution.py:249
  487.7 11.6 %convert_bitcast_fusion = f32[16,8,64,512]{3,2,1,0:T(8,128)} fusion(bf16[16,8,64,512]{3,2,1,0:T(8,128)(2,1)} %convolve.1), kind=kLoop, calls=%fused_computation.3 | loop fusion | flops 4194304 | bytes 25165824
  499.3 17.7 %copy.14 = f32[16,8,64,512]{3,1,2,0:T(8,128)} copy(f32[16,8,64,512]{3,2,1,0:T(8,128)} %convert_bitcast_fusion) | data formatting | bytes 33554432
  517.0 0.0 copy-start
  517.0 17.4 %copy.12 = f32[128,32768]{0,1:T(8,128)} copy(f32[128,32768]{1,0:T(8,128)} %bitcast.21) | data formatting | bytes 33554432 | tf_op jit(solution)/shard_map/convert_element_type | solution.py:317
  534.4 0.0 copy-done
  534.4 15.2 %fusion.1 = bf16[32768,128]{1,0:T(8,128)(2,1)} fusion(f32[128,32768]{0,1:T(8,128)} %copy.12, bf16[32768,128]{1,0:T(8,128)(2,1)} %param.4, bf16[32768,128]{1,0:T(8,128)(2,1)} %param.5, f32[128]{0:T(128)S(1)} %copy-done), kind=kLoop, calls=%fused_computation.2 | loop fusion | flops 25165824 | bytes 41943552 | tf_op jit(solution)/shard_map/convert_element_type | solution.py:319
  (1 shorter events, 0.0 us)
Async XLA Ops:
  517.0 17.4 %copy-start = (f32[128]{0:T(128)S(1)}, f32[128]{0:T(128)}, u32[]{:S(2)}) copy-start(f32[128]{0:T(128)} %param.6) | copy-start | bytes 1540

commit v2 on v1

v2 whole, which is shorter than its diff:
```python
import math

import jax
import jax.numpy as jnp
from jax import lax
from jax.experimental import pallas as pl
from jax.experimental.pallas import tpu as pltpu
from jax.sharding import PartitionSpec as P

MESH = pl.DeviceIdType.MESH
LANES = 128
GROUP = 16
PITCH = 24
STRIDE = 136
BASE = 32


def flip(me, i, shards):
    out, bit = 0, 1
    while bit < shards:
        out = out + lax.rem(lax.div(me, bit) + lax.div(i, bit), 2) * bit
        bit *= 2
    return out


def matmul(a, b):
    return lax.dot_general(a, b, (((1,), (0,)), ((), ())), preferred_element_type=jnp.float32)


def matmul_nt(a, b):
    return lax.dot_general(a, b, (((1,), (1,)), ((), ())), preferred_element_type=jnp.float32)


def circle(rows, columns, length):
    angles = 2.0 * math.pi / length * lax.rem(rows * columns, length).astype(jnp.float32)
    return jnp.cos(angles), jnp.sin(angles)


def fill(count, width, row_at, column_at, length, write):
    row = lax.broadcasted_iota(jnp.int32, (BASE, width), 0) + row_at
    column = lax.broadcasted_iota(jnp.int32, (BASE, width), 1) + column_at
    cos, sin = circle(row, column, length)
    line = lax.broadcasted_iota(jnp.int32, (1, width), 1) + column_at

    def step(i, carry):
        turn_cos, turn_sin = circle(i * BASE, line, length)
        here = pl.ds(pl.multiple_of(i * BASE, BASE), BASE)
        write(here, i, cos * turn_cos - sin * turn_sin, sin * turn_cos + cos * turn_sin)
        return carry

    lax.fori_loop(0, count // BASE, step, 0)


def convolve(signal, filt, ext, shards):
    a_loc, inner, channels = signal.shape
    d_loc, n_outer = filt.shape[1:3]
    ch_loc = channels // shards
    half = shards // 2
    d_half = half * d_loc
    f_ch = half * ch_loc
    step = 256
    chunks = n_outer // step
    groups = a_loc // GROUP
    rest = a_loc - GROUP
    d_group = min(GROUP, d_loc)
    inner_scale = 1.0 / math.sqrt(inner)
    outer_scale = 1.0 / math.sqrt(n_outer)
    ahead = min(4, ch_loc)

    def kernel(
        sig_ref, filt_ref, ext_ref, conv_ref, filt_t,
        s_buf, f_buf, e_buf, sig_t, outer_t, fwd_t, inv_t, tcb, tbc, r_buf, o_buf,
        l_buf, f_stage, turn,
        first_send, first_recv, sig_send, sig_recv, filt_send, filt_recv, ext_send, ext_recv,
        out_send, out_recv, load_sem, stage_sem,
    ):
        me = lax.axis_index("seq")
        side = lax.div(me, half)
        mine = lax.rem(me, half)
        barrier = pltpu.get_barrier_semaphore()

        def load_signal(g):
            return pltpu.make_async_copy(
                sig_ref.at[pl.ds(g * GROUP, GROUP)], l_buf.at[g % 2], load_sem.at[g % 2]
            )

        pieces = [
            (p, d, c)
            for p in range(2)
            for d in range(d_loc // d_group)
            for c in range(n_outer // inner)
        ]

        def load_filter(n):
            p, d, c = pieces[n]
            slot = (groups + n) % 2
            return pltpu.make_async_copy(
                filt_ref.at[p, pl.ds(d * d_group, d_group), pl.ds(c * inner, inner)],
                l_buf.at[slot, pl.ds(0, d_group)],
                load_sem.at[slot],
            )

        loads = [(load_signal, g) for g in range(groups)]
        loads += [(load_filter, n) for n in range(len(pieces))]

        def prefetch(n):
            if n < len(loads):
                make, at = loads[n]
                make(at).start()

        prefetch(0)
        prefetch(1)

        def greet(i, carry):
            pl.semaphore_signal(
                barrier, inc=1, device_id={"seq": lax.rem(me + i, shards)}, device_id_type=MESH
            )
            return carry

        lax.fori_loop(1, shards, greet, 0)

        def to_channels(slot, rows, first, count, store):
            def columns(j, carry):
                lanes = pl.ds(pl.multiple_of(j * LANES, LANES), LANES)
                for r in range(rows):
                    tile = l_buf[slot, r, lanes, :].astype(jnp.float32)
                    turn[pl.ds(r, channels, stride=PITCH), :] = tile.T

                def each(i, carry):
                    for n in range(8):
                        at = pl.multiple_of((first + i * 8 + n) * PITCH, 8)
                        store(i * 8 + n, lanes, turn[pl.ds(at, rows), :].astype(jnp.bfloat16))
                    return carry

                lax.fori_loop(0, count // 8, each, 0)
                return carry

            lax.fori_loop(0, inner // LANES, columns, 0)

        def turn_signal(g):
            load_signal(g).wait()

            def store(ch, lanes, tile):
                sig_t[ch, g * GROUP : (g + 1) * GROUP, lanes] = tile

            to_channels(g % 2, GROUP, 0, channels, store)
            prefetch(g + 2)

        def rows(s, skip, size):
            return pl.ds(pl.multiple_of(s * a_loc + skip, GROUP), size)

        def own(s):
            return pl.ds(pl.multiple_of(s * ch_loc, ch_loc), ch_loc)

        top = pl.ds(0, GROUP)
        below = pl.ds(GROUP, rest)
        turn_signal(0)
        pl.semaphore_wait(barrier, shards - 1)

        def send_first(i, carry):
            to = flip(me, shards - i, shards)
            pltpu.make_async_remote_copy(
                src_ref=sig_t.at[own(to), top],
                dst_ref=s_buf.at[:, rows(me, 0, GROUP)],
                send_sem=first_send,
                recv_sem=first_recv,
                device_id={"seq": to},
                device_id_type=MESH,
            ).start()
            return carry

        lax.fori_loop(1, shards, send_first, 0)
        pltpu.make_async_copy(
            sig_t.at[own(me), top], s_buf.at[:, rows(me, 0, GROUP)], first_recv
        ).start()

        @pl.when(mine == 0)
        def _():
            def send_ext(i, carry):
                to = (1 - side) * half + i
                pltpu.make_async_remote_copy(
                    src_ref=ext_ref.at[to],
                    dst_ref=e_buf,
                    send_sem=ext_send,
                    recv_sem=ext_recv,
                    device_id={"seq": to},
                    device_id_type=MESH,
                ).start()
                return carry

            lax.fori_loop(0, half, send_ext, 0)

        def send_signal(k):
            if rest == 0:
                return

            def send(i, carry):
                to = flip(me, shards - i, shards)
                pltpu.make_async_remote_copy(
                    src_ref=sig_t.at[to * ch_loc + k, below],
                    dst_ref=s_buf.at[k, rows(me, GROUP, rest)],
                    send_sem=sig_send.at[k],
                    recv_sem=sig_recv.at[k],
                    device_id={"seq": to},
                    device_id_type=MESH,
                ).start()
                return carry

            lax.fori_loop(1, shards, send, 0)
            pltpu.make_async_copy(
                sig_t.at[me * ch_loc + k, below], s_buf.at[k, rows(me, GROUP, rest)], sig_recv.at[k]
            ).start()

        def send_filter(k):
            def send(i, carry):
                to = flip(me, half - i, shards)
                pltpu.make_async_remote_copy(
                    src_ref=filt_t.at[lax.rem(to, half) * ch_loc + k],
                    dst_ref=f_buf.at[k, :, mine],
                    send_sem=filt_send.at[k],
                    recv_sem=filt_recv.at[k],
                    device_id={"seq": to},
                    device_id_type=MESH,
                ).start()
                return carry

            lax.fori_loop(1, half, send, 0)
            pltpu.make_async_copy(
                filt_t.at[mine * ch_loc + k], f_buf.at[k, :, mine], filt_recv.at[k]
            ).start()

        for g in range(1, groups):
            turn_signal(g)
        for k in range(ahead):
            send_signal(k)

        def stage(n):
            p, d, c = pieces[n]
            return pltpu.make_async_copy(
                f_stage.at[n % 2],
                filt_t.at[:, p, pl.ds(d * d_group, d_group), pl.ds(c * inner, inner)],
                stage_sem.at[n % 2],
            )

        for n in range(len(pieces)):
            load_filter(n).wait()
            if n >= 2:
                stage(n - 2).wait()

            def store(ch, lanes, tile):
                f_stage[n % 2, ch, :, lanes] = tile

            to_channels((groups + n) % 2, d_group, side * f_ch, f_ch, store)
            prefetch(groups + n + 2)
            stage(n).start()
        for n in range(max(len(pieces) - 2, 0), len(pieces)):
            stage(n).wait()
        for k in range(ahead):
            send_filter(k)

        def write_outer(here, i, cos, sin):
            outer_t[here, :] = cos.astype(jnp.bfloat16)
            low = pl.ds(pl.multiple_of(n_outer + i * BASE, BASE), BASE)
            outer_t[low, :] = (-sin).astype(jnp.bfloat16)

        def write_fwd(here, i, cos, sin):
            low = pl.ds(pl.multiple_of(d_half + i * BASE, BASE), BASE)
            fwd_t[here, 0:inner] = cos.astype(jnp.bfloat16)
            fwd_t[here, inner:] = sin.astype(jnp.bfloat16)
            fwd_t[low, 0:inner] = (-sin).astype(jnp.bfloat16)
            fwd_t[low, inner:] = cos.astype(jnp.bfloat16)

        def write_inv(here, i, cos, sin):
            low = pl.ds(pl.multiple_of(inner + i * BASE, BASE), BASE)
            inv_t[here, 0:d_half] = cos.astype(jnp.bfloat16)
            inv_t[here, d_half:] = (-sin).astype(jnp.bfloat16)
            inv_t[low, 0:d_half] = sin.astype(jnp.bfloat16)
            inv_t[low, d_half:] = cos.astype(jnp.bfloat16)

        def write_cb(here, i, cos, sin):
            tcb[0, here, :] = cos * outer_scale
            tcb[1, here, :] = sin * outer_scale

        def write_bc(here, i, cos, sin):
            tbc[0, here, :] = cos * inner_scale
            tbc[1, here, :] = sin * inner_scale

        length = n_outer * inner
        fill(n_outer, n_outer, 0, 0, n_outer, write_outer)
        fill(n_outer, inner, 0, 0, length, write_cb)
        fill(d_half, inner, side * d_half, 0, inner, write_fwd)
        fill(inner, d_half, 0, side * d_half, inner, write_inv)
        fill(inner, n_outer, 0, 0, length, write_bc)

        everything = s_buf.at[:, pl.ds(0, shards * GROUP)]
        pltpu.make_async_copy(everything, everything, first_recv).wait()
        pltpu.make_async_copy(e_buf, e_buf, ext_recv).wait()

        b_row = lax.broadcasted_iota(jnp.int32, (1, inner), 1)
        b_col = lax.broadcasted_iota(jnp.int32, (inner, 1), 0)
        swing = (1 - side).astype(jnp.float32)
        sign_row = 1.0 - 2.0 * swing * (b_row % 2).astype(jnp.float32)
        sign_col = 1.0 - 2.0 * swing * (b_col % 2).astype(jnp.float32)

        def channel(k, carry):
            slot = lax.rem(k, 2)

            @pl.when(k + ahead < ch_loc)
            def _():
                send_signal(k + ahead)
                send_filter(k + ahead)

            if rest:
                part = s_buf.at[k, pl.ds(0, shards * rest)]
                pltpu.make_async_copy(part, part, sig_recv.at[k]).wait()
            pltpu.make_async_copy(f_buf.at[k], f_buf.at[k], filt_recv.at[k]).wait()
            special = e_buf[k, :, 0:1]

            def forward(j, carry):
                at = pl.multiple_of(j * step, step)
                here = pl.ds(at, step)
                x = s_buf[k]
                f_re = matmul(outer_t[here, :], x)
                f_im = matmul(outer_t[pl.ds(pl.multiple_of(n_outer + at, step), step), :], x)
                cos, sin = tcb[0, here, :], tcb[1, here, :]
                q_re = (f_re * cos + f_im * sin).astype(jnp.bfloat16)
                q_im = (f_im * cos - f_re * sin).astype(jnp.bfloat16)
                q = jnp.concatenate([q_re, q_im], axis=1)
                spectrum = matmul_nt(fwd_t[...], q) * inner_scale
                spectrum = spectrum.astype(jnp.bfloat16).astype(jnp.float32)
                s_re, s_im = spectrum[:d_half], spectrum[d_half:]
                h_re = f_buf[k, 0, :, :, here].astype(jnp.float32).reshape(d_half, step)
                h_im = f_buf[k, 1, :, :, here].astype(jnp.float32).reshape(d_half, step)
                d_at = lax.broadcasted_iota(jnp.int32, (d_half, step), 0)
                c_at = lax.broadcasted_iota(jnp.int32, (d_half, step), 1) + at
                share = jnp.where((d_at == 0) & (c_at == 0), 0.5, 1.0)
                product = jnp.concatenate(
                    [(s_re * h_re - s_im * h_im) * share, (s_re * h_im + s_im * h_re) * share],
                    axis=0,
                ).astype(jnp.bfloat16)
                edge = jnp.sum(q_re[0:1].astype(jnp.float32) * sign_row, axis=1, keepdims=True)
                edge = (edge * inner_scale).astype(jnp.bfloat16).astype(jnp.float32)
                edge = (edge * special).astype(jnp.bfloat16).astype(jnp.float32) * 0.5
                c_row = lax.broadcasted_iota(jnp.int32, (1, step), 1) + at
                edge = jnp.where(c_row == 0, edge, 0.0)
                u = matmul(inv_t[...], product)
                u_re, u_im = u[:inner] + sign_col * edge, u[inner:]
                cos, sin = tbc[0, :, here], tbc[1, :, here]
                r_buf[0, :, here] = (u_re * cos - u_im * sin).astype(jnp.bfloat16)
                r_buf[1, :, here] = (u_re * sin + u_im * cos).astype(jnp.bfloat16)
                return carry

            lax.fori_loop(0, chunks, forward, 0)

            @pl.when(k >= 2)
            def _():
                pltpu.make_async_copy(o_buf.at[slot], o_buf.at[slot], out_send.at[slot]).wait()

            def backward(j, carry):
                at = pl.multiple_of(j * step, step)
                conv = matmul_nt(outer_t[pl.ds(at, step), :], r_buf[0]) + matmul_nt(
                    outer_t[pl.ds(pl.multiple_of(n_outer + at, step), step), :], r_buf[1]
                )
                conv = conv * (2.0 * outer_scale)
                o_buf[slot, pl.ds(at, step), :] = conv.astype(jnp.bfloat16)
                return carry

            lax.fori_loop(0, chunks, backward, 0)
            pltpu.make_async_copy(
                o_buf.at[slot, rows(me, 0, a_loc)], conv_ref.at[me, k], out_send.at[slot]
            ).start()

            def send_out(i, carry):
                to = flip(me, shards - i, shards)
                pltpu.make_async_remote_copy(
                    src_ref=o_buf.at[slot, rows(to, 0, a_loc)],
                    dst_ref=conv_ref.at[me, k],
                    send_sem=out_send.at[slot],
                    recv_sem=out_recv,
                    device_id={"seq": to},
                    device_id_type=MESH,
                ).start()
                return carry

            lax.fori_loop(1, shards, send_out, 0)
            return carry

        lax.fori_loop(0, ch_loc, channel, 0)
        for slot in range(min(2, ch_loc)):
            pltpu.make_async_copy(o_buf.at[slot], o_buf.at[slot], out_send.at[slot]).wait()
        sent = sig_t.at[pl.ds(0, (shards - 1) * ch_loc), top]
        pltpu.make_async_copy(sent, sent, first_send).wait()
        for k in range(ch_loc):
            if rest:
                sent = sig_t.at[pl.ds(0, shards - 1), pl.ds(0, rest)]
                pltpu.make_async_copy(sent, sent, sig_send.at[k]).wait()
            sent = filt_t.at[pl.ds(0, half - 1)]
            pltpu.make_async_copy(sent, sent, filt_send.at[k]).wait()

        @pl.when(mine == 0)
        def _():
            sent = ext_ref.at[pl.ds(0, half)]
            pltpu.make_async_copy(sent, sent, ext_send).wait()

        others = conv_ref.at[pl.ds(0, shards - 1)]
        pltpu.make_async_copy(others, others, out_recv).wait()

    anywhere = pl.BlockSpec(memory_space=pl.ANY)
    bf16, f32 = jnp.bfloat16, jnp.float32
    per_channel = pltpu.SemaphoreType.DMA((ch_loc,))
    single = pltpu.SemaphoreType.DMA
    pair = pltpu.SemaphoreType.DMA((2,))
    return pl.pallas_call(
        kernel,
        out_shape=(
            jax.ShapeDtypeStruct((shards, ch_loc, a_loc, inner), bf16),
            jax.ShapeDtypeStruct((f_ch, 2, d_loc, n_outer), bf16),
        ),
        in_specs=[anywhere] * 3,
        out_specs=(anywhere, anywhere),
        scratch_shapes=[
            pltpu.VMEM((ch_loc, n_outer, inner), bf16),
            pltpu.VMEM((ch_loc, 2, half, d_loc, n_outer), bf16),
            pltpu.VMEM(ext.shape[1:], f32),
            pltpu.VMEM((channels, a_loc, inner), bf16),
            pltpu.VMEM((2 * n_outer, n_outer), bf16),
            pltpu.VMEM((2 * d_half, 2 * inner), bf16),
            pltpu.VMEM((2 * inner, 2 * d_half), bf16),
            pltpu.VMEM((2, n_outer, inner), f32),
            pltpu.VMEM((2, inner, n_outer), f32),
            pltpu.VMEM((2, inner, n_outer), bf16),
            pltpu.VMEM((2, n_outer, inner), bf16),
            pltpu.VMEM((2, GROUP, inner, channels), bf16),
            pltpu.VMEM((2, f_ch, d_group, inner), bf16),
            pltpu.VMEM((channels * PITCH, LANES), f32),
            single,
            single,
            per_channel,
            per_channel,
            per_channel,
            per_channel,
            single,
            single,
            pair,
            single,
            pair,
            pair,
        ],
        compiler_params=pltpu.CompilerParams(
            collective_id=0, has_side_effects=True, vmem_limit_bytes=67043328
        ),
        name="convolve",
    )(signal, filt, ext)[0]


def finish(convolved, signal, gate, skip):
    a_loc, inner, channels = signal.shape

    def kernel(conv_ref, sig_ref, gate_ref, skip_ref, out_ref, turn):
        def each(i, carry):
            for n in range(8):
                ch = i * 8 + n
                turn[pl.ds(ch, GROUP, stride=STRIDE), :] = conv_ref[ch].astype(jnp.float32)
            return carry

        lax.fori_loop(0, channels // 8, each, 0)
        for a in range(GROUP):
            conv = turn[a * STRIDE : a * STRIDE + channels, :].T
            full = conv + skip_ref[...] * sig_ref[a].astype(jnp.float32)
            out_ref[a] = (gate_ref[a].astype(jnp.float32) * full).astype(jnp.bfloat16)

    flat = pl.BlockSpec((GROUP, LANES, channels), lambda i, j: (i, j, 0))
    return pl.pallas_call(
        kernel,
        out_shape=jax.ShapeDtypeStruct(signal.shape, jnp.bfloat16),
        grid=(a_loc // GROUP, inner // LANES),
        in_specs=[
            pl.BlockSpec((channels, GROUP, LANES), lambda i, j: (0, i, j)),
            flat,
            flat,
            pl.BlockSpec((1, channels), lambda i, j: (0, 0)),
        ],
        out_specs=flat,
        scratch_shapes=[pltpu.VMEM((GROUP * STRIDE, LANES), jnp.float32)],
        name="finish",
    )(convolved.reshape(channels, a_loc, inner), signal, gate, skip)


def local(signal, gate_values, skip_gain, filter_spectrum):
    shards = lax.axis_size("seq")
    positions, channels = signal.shape
    d_loc, n_outer = filter_spectrum.shape[1:3]
    grid = (n_outer // shards, d_loc * shards, channels)
    ch_loc = channels // shards
    ext = jnp.broadcast_to(
        filter_spectrum[0, 0, 0].astype(jnp.float32).reshape(shards, ch_loc, 1, 1),
        (shards, ch_loc, 1, LANES),
    )
    convolved = convolve(signal.reshape(grid), filter_spectrum, ext, shards)
    result = finish(
        convolved, signal.reshape(grid), gate_values.reshape(grid), skip_gain.reshape(1, channels)
    )
    return result.reshape(positions, channels)


def solution(mesh):
    return jax.shard_map(
        local,
        mesh=mesh,
        in_specs=(P("seq", "chan"), P("seq", "chan"), P("chan"), P(None, "seq", None, "chan")),
        out_specs=P("seq", "chan"),
        check_vma=False,
    )
```

time: 555 us -> 410 us (0.74)
  other arithmetic: 88.4 us -> 0.7 us
  local copies, waits for them, and re-layouts: 82.9 us -> 0.92 us
  Pallas kernels: 378 us -> 402 us
    transpose x2 -> x0, local copies, waits for them, and re-layouts: 35.4 us -> none  [the longest x1 23.5 us: local(): filter_spectrum.transpose(3, 0, 1, 2)]
    convert_element_type x3 -> x0, other arithmetic: 33.2 us -> none  [the longest x1 15.7 us: tables(): jnp.cos(angles).astype(jnp.bfloat16)]
    unnamed x4 -> x0, local copies, waits for them, and re-layouts: 27.8 us -> none
    pallas_call x1 -> x2, Pallas kernels: 378 us -> 402 us  [the longest x1 382 us: convolve(): pl.pallas_call(kernel, out_shape=(jax.ShapeDtypeStruct((shards, ch_loc, a...]
    neg x2 -> x0, other arithmetic: 17.8 us -> none  [the longest x1 15.8 us: local(): outer = jnp.concatenate([cos_a, -sin_a], 0)]
    convert_element_type x1 -> x0, local copies, waits for them, and re-layouts: 17.4 us -> none  [local(): convolved.astype(jnp.float32)]
    sin x2 -> x0, other arithmetic: 16.5 us -> none  [twiddle(): return (jnp.cos(angles), jnp.sin(angles))]
    unnamed x1 -> x0, other arithmetic: 11.6 us -> none
where the time goes in v2:
time: 410 us; the launch traced here: 403 us
  Pallas kernels  402 us (98%)
    pallas_call x1, Pallas kernels, convolve(): pl.pallas_call(kernel, out_shape=(jax.ShapeDtypeStruct((shards, ch_loc, a...  382 us
    pallas_call x1, Pallas kernels, finish(): pl.pallas_call(kernel, out_shape=jax.ShapeDtypeStruct(signal.shape, jnp.b...  19.4 us

profile of v2, /device:TPU:11, one launch (start us, length us, event | category | flops | bytes accessed | tf_op | source)
XLA Modules:
  0.0 403.4 jit_solution(14085933480963608185)
XLA Ops:
  0.0 0.7 convert_reduce_fusion
  0.7 0.1 reshape.31
  0.8 0.8 broadcast_in_dim.2.ext_ref
  1.6 382.3 %convolve.1 = (bf16[16,8,64,512]{3,2,1,0:T(8,128)(2,1)}, bf16[64,2,32,1024]{3,2,1,0:T(8,128)(2,1)}) custom-call(bf16[64,512,128]{2,1,0:T(8,128)(2,1)} %bitcast.5, bf16[2,32,1024,128]{3,2,1,0:T(8,128)(2,1)} %filt_ref.1, f32[16,8,1,128]{3,2,1,0:T(1,128)} %broadcast_in_dim.2.ext_ref), custom_call_target="tpu_custom_call" | custom-call | tf_op jit(solution)/shard_map/convolve/pallas_call | solution.py:413
  383.9 19.4 %finish.1 = bf16[64,512,128]{2,1,0:T(8,128)(2,1)} custom-call(bf16[128,64,512]{2,1,0:T(8,128)(2,1)} %bitcast.8, bf16[64,512,128]{2,1,0:T(8,128)(2,1)} %bitcast.6, bf16[64,512,128]{2,1,0:T(8,128)(2,1)} %bitcast.7, f32[1,128]{1,0:T(1,128)} %bitcast.9), custom_call_target="tpu_custom_call" | custom-call | tf_op jit(solution)/shard_map/finish/pallas_call | solution.py:473

commit v3 on v2

--- a/solution.py
+++ b/solution.py
@@ -51,7 +51,21 @@
     lax.fori_loop(0, count // BASE, step, 0)
 
 
-def convolve(signal, filt, ext, shards):
+def to_positions(turn, shards, ch_loc, load, store):
+    channels = shards * ch_loc
+
+    def each(t, carry):
+        for k in range(ch_loc):
+            at = t * ch_loc + k
+            turn[pl.ds(at, GROUP, stride=STRIDE), :] = load(t, k).astype(jnp.float32)
+        return carry
+
+    lax.fori_loop(0, shards, each, 0)
+    for a in range(GROUP):
+        store(a, turn[a * STRIDE : a * STRIDE + channels, :].T)
+
+
+def convolve(signal, gate, skip, filt, ext, shards):
     a_loc, inner, channels = signal.shape
     d_loc, n_outer = filt.shape[1:3]
     ch_loc = channels // shards
@@ -65,14 +79,14 @@
     d_group = min(GROUP, d_loc)
     inner_scale = 1.0 / math.sqrt(inner)
     outer_scale = 1.0 / math.sqrt(n_outer)
-    ahead = min(4, ch_loc)
+    ahead = min(2, ch_loc)
 
     def kernel(
-        sig_ref, filt_ref, ext_ref, conv_ref, filt_t,
+        sig_ref, gate_ref, skip_ref, filt_ref, ext_ref, conv_ref, filt_t, part_ref,
         s_buf, f_buf, e_buf, sig_t, outer_t, fwd_t, inv_t, tcb, tbc, r_buf, o_buf,
-        l_buf, f_stage, turn,
+        l_buf, f_stage, turn, c_buf,
         first_send, first_recv, sig_send, sig_recv, filt_send, filt_recv, ext_send, ext_recv,
-        out_send, out_recv, load_sem, stage_sem,
+        out_send, out_own, out_recv, end_recv, load_sem, stage_sem, tail_sem, part_sem,
     ):
         me = lax.axis_index("seq")
         side = lax.div(me, half)
@@ -149,6 +163,9 @@
         def rows(s, skip, size):
             return pl.ds(pl.multiple_of(s * a_loc + skip, GROUP), size)
 
+        def group_rows(g):
+            return pl.ds(pl.multiple_of(g * GROUP, GROUP), GROUP)
+
         def own(s):
             return pl.ds(pl.multiple_of(s * ch_loc, ch_loc), ch_loc)
 
@@ -157,8 +174,10 @@
         turn_signal(0)
         pl.semaphore_wait(barrier, shards - 1)
 
+        parity = lax.rem(me, 2)
+
         def send_first(i, carry):
-            to = flip(me, shards - i, shards)
+            to = flip(me, (1 - parity) * (shards - i) + parity * i, shards)
             pltpu.make_async_remote_copy(
                 src_ref=sig_t.at[own(to), top],
                 dst_ref=s_buf.at[:, rows(me, 0, GROUP)],
@@ -190,12 +209,33 @@
 
             lax.fori_loop(0, half, send_ext, 0)
 
-        def send_signal(k):
-            if rest == 0:
-                return
-
-            def send(i, carry):
-                to = flip(me, shards - i, shards)
+        quarter = half // 2
+
+        def ordered(far, near, middle=None):
+            def far_loop():
+                def one(n, carry):
+                    far(half + (1 - lax.rem(n, 2)) * quarter + lax.div(n, 2))
+                    return carry
+
+                lax.fori_loop(0, half, one, 0)
+
+            def near_loop(send, low, high):
+                def one(i, carry):
+                    send(i)
+                    return carry
+
+                lax.fori_loop(low, high, one, 0)
+
+            pl.when(parity == 0)(far_loop)
+            for low, high in ((quarter, half), (1, quarter)):
+                if middle is not None:
+                    near_loop(middle, low, high)
+                near_loop(near, low, high)
+            pl.when(parity == 1)(far_loop)
+
+        def send_round(k):
+            def send_signal(i):
+                to = flip(me, i, shards)
                 pltpu.make_async_remote_copy(
                     src_ref=sig_t.at[to * ch_loc + k, below],
                     dst_ref=s_buf.at[k, rows(me, GROUP, rest)],
@@ -204,16 +244,9 @@
                     device_id={"seq": to},
                     device_id_type=MESH,
                 ).start()
-                return carry
-
-            lax.fori_loop(1, shards, send, 0)
-            pltpu.make_async_copy(
-                sig_t.at[me * ch_loc + k, below], s_buf.at[k, rows(me, GROUP, rest)], sig_recv.at[k]
-            ).start()
-
-        def send_filter(k):
-            def send(i, carry):
-                to = flip(me, half - i, shards)
+
+            def send_filter(i):
+                to = flip(me, i, shards)
                 pltpu.make_async_remote_copy(
                     src_ref=filt_t.at[lax.rem(to, half) * ch_loc + k],
                     dst_ref=f_buf.at[k, :, mine],
@@ -222,18 +255,24 @@
                     device_id={"seq": to},
                     device_id_type=MESH,
                 ).start()
-                return carry
-
-            lax.fori_loop(1, half, send, 0)
+
+            def nothing(i):
+                return None
+
+            signal_step = send_signal if rest else nothing
+            ordered(signal_step, signal_step, send_filter)
+            if rest:
+                pltpu.make_async_copy(
+                    sig_t.at[me * ch_loc + k, below],
+                    s_buf.at[k, rows(me, GROUP, rest)],
+                    sig_recv.at[k],
+                ).start()
             pltpu.make_async_copy(
                 filt_t.at[mine * ch_loc + k], f_buf.at[k, :, mine], filt_recv.at[k]
             ).start()
 
         for g in range(1, groups):
             turn_signal(g)
-        for k in range(ahead):
-            send_signal(k)
-
         def stage(n):
             p, d, c = pieces[n]
             return pltpu.make_async_copy(
@@ -256,7 +295,7 @@
         for n in range(max(len(pieces) - 2, 0), len(pieces)):
             stage(n).wait()
         for k in range(ahead):
-            send_filter(k)
+            send_round(k)
 
         def write_outer(here, i, cos, sin):
             outer_t[here, :] = cos.astype(jnp.bfloat16)
@@ -305,16 +344,16 @@
         def channel(k, carry):
             slot = lax.rem(k, 2)
 
-            @pl.when(k + ahead < ch_loc)
-            def _():
-                send_signal(k + ahead)
-                send_filter(k + ahead)
-
             if rest:
                 part = s_buf.at[k, pl.ds(0, shards * rest)]
                 pltpu.make_async_copy(part, part, sig_recv.at[k]).wait()
             pltpu.make_async_copy(f_buf.at[k], f_buf.at[k], filt_recv.at[k]).wait()
             special = e_buf[k, :, 0:1]
+
+            @pl.when(k + ahead < ch_loc)
+            def _():
+                send_round(k + ahead)
+
 
             def forward(j, carry):
                 at = pl.multiple_of(j * step, step)
@@ -354,7 +393,10 @@
 
             @pl.when(k >= 2)
             def _():
-                pltpu.make_async_copy(o_buf.at[slot], o_buf.at[slot], out_send.at[slot]).wait()
+                sent = o_buf.at[slot, pl.ds(0, (shards - 1) * a_loc)]
+                pltpu.make_async_copy(sent, sent, out_send.at[slot]).wait()
+                kept = o_buf.at[slot, pl.ds(0, a_loc)]
+                pltpu.make_async_copy(kept, kept, out_own.at[slot]).wait()
 
             def backward(j, carry):
                 at = pl.multiple_of(j * step, step)
@@ -367,11 +409,11 @@
 
             lax.fori_loop(0, chunks, backward, 0)
             pltpu.make_async_copy(
-                o_buf.at[slot, rows(me, 0, a_loc)], conv_ref.at[me, k], out_send.at[slot]
+                o_buf.at[slot, rows(me, 0, a_loc)], conv_ref.at[me, k], out_own.at[slot]
             ).start()
 
-            def send_out(i, carry):
-                to = flip(me, shards - i, shards)
+            def send_out(i):
+                to = flip(me, i, shards)
                 pltpu.make_async_remote_copy(
                     src_ref=o_buf.at[slot, rows(to, 0, a_loc)],
                     dst_ref=conv_ref.at[me, k],
@@ -380,14 +422,92 @@
                     device_id={"seq": to},
                     device_id_type=MESH,
                 ).start()
+
+            def send_end(g, carry):
+                def send(i):
+                    to = flip(me, i, shards)
+                    pltpu.make_async_remote_copy(
+                        src_ref=o_buf.at[slot, rows(to, g * GROUP, GROUP)],
+                        dst_ref=conv_ref.at[me, k, group_rows(g)],
+                        send_sem=out_send.at[slot],
+                        recv_sem=end_recv.at[g],
+                        device_id={"seq": to},
+                        device_id_type=MESH,
+                    ).start()
+
+                ordered(send, send)
                 return carry
 
-            lax.fori_loop(1, shards, send_out, 0)
+            @pl.when(k < ch_loc - 1)
+            def _():
+                ordered(send_out, send_out)
+
+            @pl.when(k == ch_loc - 1)
+            def _():
+                lax.fori_loop(0, groups, send_end, 0)
+
             return carry
 
+        def tail_load(g):
+            lane = 2 * (g % 2)
+            return [
+                pltpu.make_async_copy(ref.at[group_rows(g)], l_buf.at[lane + i], tail_sem.at[lane + i])
+                for i, ref in enumerate((sig_ref, gate_ref))
+            ]
+
+        def tail_store(g):
+            return pltpu.make_async_copy(
+                l_buf.at[2 * (g % 2) + 1], part_ref.at[group_rows(g)], part_sem.at[g % 2]
+            )
+
+        for g in range(min(2, groups - 1)):
+            for copy in tail_load(g):
+                copy.start()
         lax.fori_loop(0, ch_loc, channel, 0)
-        for slot in range(min(2, ch_loc)):
-            pltpu.make_async_copy(o_buf.at[slot], o_buf.at[slot], out_send.at[slot]).wait()
+        for k in range(max(ch_loc - 2, 0), ch_loc):
+            kept = o_buf.at[k % 2, pl.ds(0, a_loc)]
+            pltpu.make_async_copy(kept, kept, out_own.at[k % 2]).wait()
+        if ch_loc > 1:
+            others = conv_ref.at[pl.ds(0, shards - 1), pl.ds(0, ch_loc - 1)]
+            pltpu.make_async_copy(others, others, out_recv).wait()
+
+        for g in range(groups):
+            landed = conv_ref.at[pl.ds(0, shards - 1), 0, pl.ds(0, GROUP)]
+            pltpu.make_async_copy(landed, landed, end_recv.at[g]).wait()
+            if g == groups - 1:
+                break
+            fetch = pltpu.make_async_copy(conv_ref.at[:, :, group_rows(g)], c_buf, tail_sem.at[4])
+            fetch.start()
+            for copy in tail_load(g):
+                copy.wait()
+            fetch.wait()
+            lane = 2 * (g % 2)
+
+            def columns(j, carry):
+                lanes = pl.ds(pl.multiple_of(j * LANES, LANES), LANES)
+
+                def load(t, k):
+                    return c_buf[t, k, :, lanes]
+
+                def store(a, conv):
+                    full = conv + skip_ref[...] * l_buf[lane, a, lanes, :].astype(jnp.float32)
+                    full = l_buf[lane + 1, a, lanes, :].astype(jnp.float32) * full
+                    l_buf[lane + 1, a, lanes, :] = full.astype(jnp.bfloat16)
+
+                to_positions(turn, shards, ch_loc, load, store)
+                return carry
+
+            lax.fori_loop(0, inner // LANES, columns, 0)
+            tail_store(g).start()
+            if g + 2 < groups - 1:
+                tail_store(g).wait()
+                for copy in tail_load(g + 2):
+                    copy.start()
+        for g in range(max(groups - 3, 0), groups - 1):
+            tail_store(g).wait()
+        for k in range(max(ch_loc - 2, 0), ch_loc):
+            sent = o_buf.at[k % 2, pl.ds(0, (shards - 1) * a_loc)]
+            pltpu.make_async_copy(sent, sent, out_send.at[k % 2]).wait()
         sent = sig_t.at[pl.ds(0, (shards - 1) * ch_loc), top]
         pltpu.make_async_copy(sent, sent, first_send).wait()
         for k in range(ch_loc):
@@ -401,9 +521,6 @@
         def _():
             sent = ext_ref.at[pl.ds(0, half)]
             pltpu.make_async_copy(sent, sent, ext_send).wait()
-
-        others = conv_ref.at[pl.ds(0, shards - 1)]
-        pltpu.make_async_copy(others, others, out_recv).wait()
 
     anywhere = pl.BlockSpec(memory_space=pl.ANY)
     bf16, f32 = jnp.bfloat16, jnp.float32
@@ -415,9 +532,10 @@
         out_shape=(
             jax.ShapeDtypeStruct((shards, ch_loc, a_loc, inner), bf16),
             jax.ShapeDtypeStruct((f_ch, 2, d_loc, n_outer), bf16),
+            jax.ShapeDtypeStruct((max(rest, GROUP), inner, channels), bf16),
         ),
-        in_specs=[anywhere] * 3,
-        out_specs=(anywhere, anywhere),
+        in_specs=[anywhere, anywhere, pl.BlockSpec(memory_space=pltpu.VMEM), anywhere, anywhere],
+        out_specs=(anywhere, anywhere, anywhere),
         scratch_shapes=[
             pltpu.VMEM((ch_loc, n_outer, inner), bf16),
             pltpu.VMEM((ch_loc, 2, half, d_loc, n_outer), bf16),
@@ -430,9 +548,10 @@
             pltpu.VMEM((2, inner, n_outer), f32),
             pltpu.VMEM((2, inner, n_outer), bf16),
             pltpu.VMEM((2, n_outer, inner), bf16),
-            pltpu.VMEM((2, GROUP, inner, channels), bf16),
+            pltpu.VMEM((4, GROUP, inner, channels), bf16),
             pltpu.VMEM((2, f_ch, d_group, inner), bf16),
             pltpu.VMEM((channels * PITCH, LANES), f32),
+            pltpu.VMEM((shards, ch_loc, GROUP, inner), bf16),
             single,
             single,
             per_channel,
@@ -442,48 +561,100 @@
             single,
             single,
             pair,
+            pair,
             single,
+            pltpu.SemaphoreType.DMA((groups,)),
             pair,
+            pair,
+            pltpu.SemaphoreType.DMA((5,)),
             pair,
         ],
         compiler_params=pltpu.CompilerParams(
             collective_id=0, has_side_effects=True, vmem_limit_bytes=67043328
         ),
         name="convolve",
-    )(signal, filt, ext)[0]
-
-
-def finish(convolved, signal, gate, skip):
+    )(signal, gate, skip, filt, ext)
+
+
+def finish(convolved, part, signal, gate, skip):
     a_loc, inner, channels = signal.shape
-
-    def kernel(conv_ref, sig_ref, gate_ref, skip_ref, out_ref, turn):
-        def each(i, carry):
-            for n in range(8):
-                ch = i * 8 + n
-                turn[pl.ds(ch, GROUP, stride=STRIDE), :] = conv_ref[ch].astype(jnp.float32)
-            return carry
-
-        lax.fori_loop(0, channels // 8, each, 0)
-        for a in range(GROUP):
-            conv = turn[a * STRIDE : a * STRIDE + channels, :].T
-            full = conv + skip_ref[...] * sig_ref[a].astype(jnp.float32)
-            out_ref[a] = (gate_ref[a].astype(jnp.float32) * full).astype(jnp.bfloat16)
-
-    flat = pl.BlockSpec((GROUP, LANES, channels), lambda i, j: (i, j, 0))
+    shards, ch_loc = convolved.shape[:2]
+    done = a_loc - GROUP
+    copies = done // GROUP
+    chunks = inner // LANES
+
+    def kernel(
+        conv_ref, part_ref, sig_ref, gate_ref, skip_ref, out_ref,
+        c_buf, s_buf, g_buf, p_buf, turn, in_sem, part_in, part_out, out_sem,
+    ):
+        last = pl.ds(done, GROUP)
+        loads = [
+            pltpu.make_async_copy(conv_ref.at[:, :, last], c_buf, in_sem.at[0]),
+            pltpu.make_async_copy(sig_ref.at[last], s_buf, in_sem.at[1]),
+            pltpu.make_async_copy(gate_ref.at[last], g_buf, in_sem.at[2]),
+        ]
+        moves = []
+        for n in range(copies):
+            rows = pl.ds(n * GROUP, GROUP)
+            moves.append(
+                (
+                    pltpu.make_async_copy(part_ref.at[rows], p_buf.at[n], part_in.at[n]),
+                    pltpu.make_async_copy(p_buf.at[n], out_ref.at[rows], part_out.at[n]),
+                )
+            )
+        for copy in loads + [move[0] for move in moves]:
+            copy.start()
+        for copy in loads:
+            copy.wait()
+        stores = []
+        for j in range(chunks):
+            lanes = pl.ds(j * LANES, LANES)
+
+            def load(t, k):
+                return c_buf[t, k, :, lanes]
+
+            def store(a, conv):
+                full = conv + skip_ref[...] * s_buf[a, lanes, :].astype(jnp.float32)
+                full = g_buf[a, lanes, :].astype(jnp.float32) * full
+                g_buf[a, lanes, :] = full.astype(jnp.bfloat16)
+
+            to_positions(turn, shards, ch_loc, load, store)
+            stores.append(
+                pltpu.make_async_copy(
+                    g_buf.at[:, lanes], out_ref.at[last, lanes], out_sem.at[j]
+                )
+            )
+            stores[-1].start()
+            if j < copies:
+                moves[j][0].wait()
+                moves[j][1].start()
+        for n in range(chunks, copies):
+            moves[n][0].wait()
+            moves[n][1].start()
+        for copy in stores + [move[1] for move in moves]:
+            copy.wait()
+
+    anywhere = pl.BlockSpec(memory_space=pl.ANY)
+    rows_shape = (GROUP, inner, channels)
     return pl.pallas_call(
         kernel,
         out_shape=jax.ShapeDtypeStruct(signal.shape, jnp.bfloat16),
-        grid=(a_loc // GROUP, inner // LANES),
-        in_specs=[
-            pl.BlockSpec((channels, GROUP, LANES), lambda i, j: (0, i, j)),
-            flat,
-            flat,
-            pl.BlockSpec((1, channels), lambda i, j: (0, 0)),
+        in_specs=[anywhere] * 4 + [pl.BlockSpec(memory_space=pltpu.VMEM)],
+        out_specs=anywhere,
+        scratch_shapes=[
+            pltpu.VMEM((shards, ch_loc, GROUP, inner), jnp.bfloat16),
+            pltpu.VMEM(rows_shape, jnp.bfloat16),
+            pltpu.VMEM(rows_shape, jnp.bfloat16),
+            pltpu.VMEM((max(copies, 1), *rows_shape), jnp.bfloat16),
+            pltpu.VMEM((GROUP * STRIDE, LANES), jnp.float32),
+            pltpu.SemaphoreType.DMA((3,)),
+            pltpu.SemaphoreType.DMA((max(copies, 1),)),
+            pltpu.SemaphoreType.DMA((max(copies, 1),)),
+            pltpu.SemaphoreType.DMA((chunks,)),
         ],
-        out_specs=flat,
-        scratch_shapes=[pltpu.VMEM((GROUP * STRIDE, LANES), jnp.float32)],
+        compiler_params=pltpu.CompilerParams(vmem_limit_bytes=67043328),
         name="finish",
-    )(convolved.reshape(channels, a_loc, inner), signal, gate, skip)
+    )(convolved, part, signal, gate, skip)
 
 
 def local(signal, gate_values, skip_gain, filter_spectrum):
@@ -496,10 +667,10 @@
         filter_spectrum[0, 0, 0].astype(jnp.float32).reshape(shards, ch_loc, 1, 1),
         (shards, ch_loc, 1, LANES),
     )
-    convolved = convolve(signal.reshape(grid), filter_spectrum, ext, shards)
-    result = finish(
-        convolved, signal.reshape(grid), gate_values.reshape(grid), skip_gain.reshape(1, channels)
-    )
+    signal, gate = signal.reshape(grid), gate_values.reshape(grid)
+    skip = skip_gain.reshape(1, channels)
+    convolved, _, part = convolve(signal, gate, skip, filter_spectrum, ext, shards)
+    result = finish(convolved, part, signal, gate, skip)
     return result.reshape(positions, channels)
 
 

time: 410 us -> 387 us (0.944)
  Pallas kernels: 402 us -> 382 us
    pallas_call x1, Pallas kernels: 19.4 us -> 8.75 us  [finish(): pl.pallas_call(kernel, out_shape=jax.ShapeDtypeStruct(signal.shape, jnp.b...]
    pallas_call x1, Pallas kernels: 382 us -> 373 us  [convolve(): pl.pallas_call(kernel, out_shape=(jax.ShapeDtypeStruct((shards, ch_loc, a...]
where the time goes in v3:
time: 387 us; the launch traced here: 384 us
  Pallas kernels  382 us (99%)
    pallas_call x1, Pallas kernels, convolve(): pl.pallas_call(kernel, out_shape=(jax.ShapeDtypeStruct((shards, ch_loc, a...  373 us
    pallas_call x1, Pallas kernels, finish(): pl.pallas_call(kernel, out_shape=jax.ShapeDtypeStruct(signal.shape, jnp.b...  8.75 us

profile of v3, /device:TPU:11, one launch (start us, length us, event | category | flops | bytes accessed | tf_op | source)
XLA Modules:
  0.0 383.6 jit_solution(10660402751158637818)
XLA Ops:
  0.0 0.7 convert_reduce_fusion
  0.7 0.1 reshape.26
  0.8 0.8 broadcast_in_dim.2.ext_ref
  1.6 373.2 %convolve.1 = (bf16[16,8,64,512]{3,2,1,0:T(8,128)(2,1)}, bf16[64,2,32,1024]{3,2,1,0:T(8,128)(2,1)}, bf16[48,512,128]{2,1,0:T(8,128)(2,1)}) custom-call(bf16[64,512,128]{2,1,0:T(8,128)(2,1)} %bitcast.4, bf16[64,512,128]{2,1,0:T(8,128)(2,1)} %bitcast.6, f32[1,128]{1,0:T(1,128)} %bitcast.8, bf16[2,32,1024,128]{3,2,1,0:T(8,128)(2,1)} %filt_ref.1, ...), custom_call_target="tpu_custom_call" | custom-call | tf_op jit(solution)/shard_map/convolve/pallas_call | solution.py:530
  374.9 8.7 %finish.1 = bf16[64,512,128]{2,1,0:T(8,128)(2,1)} custom-call(bf16[16,8,64,512]{3,2,1,0:T(8,128)(2,1)} %get-tuple-element.7.conv_ref, bf16[48,512,128]{2,1,0:T(8,128)(2,1)} %get-tuple-element.8.part_ref, bf16[64,512,128]{2,1,0:T(8,128)(2,1)} %bitcast.5, bf16[64,512,128]{2,1,0:T(8,128)(2,1)} %bitcast.7, f32[1,128]{1,0:T(1,128)} %bitcast.9), custom_call_target="tpu_custom_call" | custom-call | tf_op jit(solution)/shard_map/finish/pallas_call | solution.py:639

commit v4 on v3

--- a/solution.py
+++ b/solution.py
@@ -65,7 +65,7 @@
         store(a, turn[a * STRIDE : a * STRIDE + channels, :].T)
 
 
-def convolve(signal, gate, skip, filt, ext, shards):
+def convolve(signal, gate, skip, filt, shards):
     a_loc, inner, channels = signal.shape
     d_loc, n_outer = filt.shape[1:3]
     ch_loc = channels // shards
@@ -82,7 +82,7 @@
     ahead = min(2, ch_loc)
 
     def kernel(
-        sig_ref, gate_ref, skip_ref, filt_ref, ext_ref, conv_ref, filt_t, part_ref,
+        sig_ref, gate_ref, skip_ref, filt_ref, conv_ref, filt_t, part_ref,
         s_buf, f_buf, e_buf, sig_t, outer_t, fwd_t, inv_t, tcb, tbc, r_buf, o_buf,
         l_buf, f_stage, turn, c_buf,
         first_send, first_recv, sig_send, sig_recv, filt_send, filt_recv, ext_send, ext_recv,
@@ -133,7 +133,7 @@
 
         lax.fori_loop(1, shards, greet, 0)
 
-        def to_channels(slot, rows, first, count, store):
+        def to_channels(slot, rows, first, count, store, low=0, high=inner // LANES):
             def columns(j, carry):
                 lanes = pl.ds(pl.multiple_of(j * LANES, LANES), LANES)
                 for r in range(rows):
@@ -149,7 +149,7 @@
                 lax.fori_loop(0, count // 8, each, 0)
                 return carry
 
-            lax.fori_loop(0, inner // LANES, columns, 0)
+            lax.fori_loop(low, high, columns, 0)
 
         def turn_signal(g):
             load_signal(g).wait()
@@ -169,26 +169,38 @@
         def own(s):
             return pl.ds(pl.multiple_of(s * ch_loc, ch_loc), ch_loc)
 
+        edge_rows = pl.ds(0, GROUP)
         top = pl.ds(0, GROUP)
         below = pl.ds(GROUP, rest)
-        turn_signal(0)
-        pl.semaphore_wait(barrier, shards - 1)
-
         parity = lax.rem(me, 2)
-
-        def send_first(i, carry):
-            to = flip(me, (1 - parity) * (shards - i) + parity * i, shards)
-            pltpu.make_async_remote_copy(
-                src_ref=sig_t.at[own(to), top],
-                dst_ref=s_buf.at[:, rows(me, 0, GROUP)],
-                send_sem=first_send,
-                recv_sem=first_recv,
-                device_id={"seq": to},
-                device_id_type=MESH,
-            ).start()
-            return carry
-
-        lax.fori_loop(1, shards, send_first, 0)
+        parts = 2
+        width = inner // parts
+
+        def store_first(ch, lanes, tile):
+            sig_t[ch, 0:GROUP, lanes] = tile
+
+        load_signal(0).wait()
+        for part in range(parts):
+            block = pl.ds(part * width, width)
+
+            def send_first(i, carry):
+                to = flip(me, (1 - parity) * (shards - i) + parity * i, shards)
+                pltpu.make_async_remote_copy(
+                    src_ref=sig_t.at[own(to), top, block],
+                    dst_ref=s_buf.at[:, rows(me, 0, GROUP), block],
+                    send_sem=first_send,
+                    recv_sem=first_recv,
+                    device_id={"seq": to},
+                    device_id_type=MESH,
+                ).start()
+                return carry
+
+            tiles = width // LANES
+            to_channels(0, GROUP, 0, channels, store_first, part * tiles, (part + 1) * tiles)
+            if part == 0:
+                pl.semaphore_wait(barrier, shards - 1)
+            lax.fori_loop(1, shards, send_first, 0)
+        prefetch(2)
         pltpu.make_async_copy(
             sig_t.at[own(me), top], s_buf.at[:, rows(me, 0, GROUP)], first_recv
         ).start()
@@ -198,7 +210,7 @@
             def send_ext(i, carry):
                 to = (1 - side) * half + i
                 pltpu.make_async_remote_copy(
-                    src_ref=ext_ref.at[to],
+                    src_ref=filt_ref.at[0, 0, edge_rows],
                     dst_ref=e_buf,
                     send_sem=ext_send,
                     recv_sem=ext_recv,
@@ -211,10 +223,10 @@
 
         quarter = half // 2
 
-        def ordered(far, near, middle=None):
+        def ordered(far, near, middle=None, eager=None):
             def far_loop():
                 def one(n, carry):
-                    far(half + (1 - lax.rem(n, 2)) * quarter + lax.div(n, 2))
+                    far(half + lax.rem(n, 2) * quarter + lax.div(n, 2))
                     return carry
 
                 lax.fori_loop(0, half, one, 0)
@@ -226,12 +238,13 @@
 
                 lax.fori_loop(low, high, one, 0)
 
-            pl.when(parity == 0)(far_loop)
+            eager = parity == 0 if eager is None else eager
+            pl.when(eager)(far_loop)
             for low, high in ((quarter, half), (1, quarter)):
                 if middle is not None:
                     near_loop(middle, low, high)
                 near_loop(near, low, high)
-            pl.when(parity == 1)(far_loop)
+            pl.when(jnp.logical_not(eager))(far_loop)
 
         def send_round(k):
             def send_signal(i):
@@ -334,6 +347,7 @@
         everything = s_buf.at[:, pl.ds(0, shards * GROUP)]
         pltpu.make_async_copy(everything, everything, first_recv).wait()
         pltpu.make_async_copy(e_buf, e_buf, ext_recv).wait()
+        e_row = e_buf[...].astype(jnp.float32)[0:1]
 
         b_row = lax.broadcasted_iota(jnp.int32, (1, inner), 1)
         b_col = lax.broadcasted_iota(jnp.int32, (inner, 1), 0)
@@ -348,7 +362,9 @@
                 part = s_buf.at[k, pl.ds(0, shards * rest)]
                 pltpu.make_async_copy(part, part, sig_recv.at[k]).wait()
             pltpu.make_async_copy(f_buf.at[k], f_buf.at[k], filt_recv.at[k]).wait()
-            special = e_buf[k, :, 0:1]
+            e_lane = lax.broadcasted_iota(jnp.int32, (1, channels), 1)
+            special = jnp.where(e_lane == me * ch_loc + k, e_row, 0.0)
+            special = jnp.sum(special, axis=1, keepdims=True)
 
             @pl.when(k + ahead < ch_loc)
             def _():
@@ -435,12 +451,12 @@
                         device_id_type=MESH,
                     ).start()
 
-                ordered(send, send)
+                ordered(send, send, eager=k >= 0)
                 return carry
 
             @pl.when(k < ch_loc - 1)
             def _():
-                ordered(send_out, send_out)
+                ordered(send_out, send_out, eager=(parity == 0) | (k >= ch_loc // 2 + 1))
 
             @pl.when(k == ch_loc - 1)
             def _():
@@ -519,7 +535,7 @@
 
         @pl.when(mine == 0)
         def _():
-            sent = ext_ref.at[pl.ds(0, half)]
+            sent = filt_ref.at[0, 0, pl.ds(0, half * GROUP)]
             pltpu.make_async_copy(sent, sent, ext_send).wait()
 
     anywhere = pl.BlockSpec(memory_space=pl.ANY)
@@ -534,12 +550,12 @@
             jax.ShapeDtypeStruct((f_ch, 2, d_loc, n_outer), bf16),
             jax.ShapeDtypeStruct((max(rest, GROUP), inner, channels), bf16),
         ),
-        in_specs=[anywhere, anywhere, pl.BlockSpec(memory_space=pltpu.VMEM), anywhere, anywhere],
+        in_specs=[anywhere, anywhere, pl.BlockSpec(memory_space=pltpu.VMEM), anywhere],
         out_specs=(anywhere, anywhere, anywhere),
         scratch_shapes=[
             pltpu.VMEM((ch_loc, n_outer, inner), bf16),
             pltpu.VMEM((ch_loc, 2, half, d_loc, n_outer), bf16),
-            pltpu.VMEM(ext.shape[1:], f32),
+            pltpu.VMEM((GROUP, channels), bf16),
             pltpu.VMEM((channels, a_loc, inner), bf16),
             pltpu.VMEM((2 * n_outer, n_outer), bf16),
             pltpu.VMEM((2 * d_half, 2 * inner), bf16),
@@ -573,7 +589,7 @@
             collective_id=0, has_side_effects=True, vmem_limit_bytes=67043328
         ),
         name="convolve",
-    )(signal, gate, skip, filt, ext)
+    )(signal, gate, skip, filt)
 
 
 def finish(convolved, part, signal, gate, skip):
@@ -588,11 +604,24 @@
         c_buf, s_buf, g_buf, p_buf, turn, in_sem, part_in, part_out, out_sem,
     ):
         last = pl.ds(done, GROUP)
-        loads = [
-            pltpu.make_async_copy(conv_ref.at[:, :, last], c_buf, in_sem.at[0]),
-            pltpu.make_async_copy(sig_ref.at[last], s_buf, in_sem.at[1]),
-            pltpu.make_async_copy(gate_ref.at[last], g_buf, in_sem.at[2]),
-        ]
+        loads = []
+        for j in range(chunks):
+            lanes = pl.ds(j * LANES, LANES)
+            loads.append(
+                [
+                    pltpu.make_async_copy(
+                        conv_ref.at[:, :, last, lanes], c_buf.at[:, :, :, lanes], in_sem.at[0, j]
+                    ),
+                    pltpu.make_async_copy(
+                        sig_ref.at[last, lanes], s_buf.at[:, lanes], in_sem.at[1, j]
+                    ),
+                    pltpu.make_async_copy(
+                        gate_ref.at[last, lanes], g_buf.at[:, lanes], in_sem.at[2, j]
+                    ),
+                ]
+            )
+            for copy in loads[-1]:
+                copy.start()
         moves = []
         for n in range(copies):
             rows = pl.ds(n * GROUP, GROUP)
@@ -602,10 +631,6 @@
                     pltpu.make_async_copy(p_buf.at[n], out_ref.at[rows], part_out.at[n]),
                 )
             )
-        for copy in loads + [move[0] for move in moves]:
-            copy.start()
-        for copy in loads:
-            copy.wait()
         stores = []
         for j in range(chunks):
             lanes = pl.ds(j * LANES, LANES)
@@ -618,6 +643,11 @@
                 full = g_buf[a, lanes, :].astype(jnp.float32) * full
                 g_buf[a, lanes, :] = full.astype(jnp.bfloat16)
 
+            for copy in loads[j]:
+                copy.wait()
+            if j == 0:
+                for move in moves:
+                    move[0].start()
             to_positions(turn, shards, ch_loc, load, store)
             stores.append(
                 pltpu.make_async_copy(
@@ -647,7 +677,7 @@
             pltpu.VMEM(rows_shape, jnp.bfloat16),
             pltpu.VMEM((max(copies, 1), *rows_shape), jnp.bfloat16),
             pltpu.VMEM((GROUP * STRIDE, LANES), jnp.float32),
-            pltpu.SemaphoreType.DMA((3,)),
+            pltpu.SemaphoreType.DMA((3, chunks)),
             pltpu.SemaphoreType.DMA((max(copies, 1),)),
             pltpu.SemaphoreType.DMA((max(copies, 1),)),
             pltpu.SemaphoreType.DMA((chunks,)),
@@ -662,14 +692,9 @@
     positions, channels = signal.shape
     d_loc, n_outer = filter_spectrum.shape[1:3]
     grid = (n_outer // shards, d_loc * shards, channels)
-    ch_loc = channels // shards
-    ext = jnp.broadcast_to(
-        filter_spectrum[0, 0, 0].astype(jnp.float32).reshape(shards, ch_loc, 1, 1),
-        (shards, ch_loc, 1, LANES),
-    )
     signal, gate = signal.reshape(grid), gate_values.reshape(grid)
     skip = skip_gain.reshape(1, channels)
-    convolved, _, part = convolve(signal, gate, skip, filter_spectrum, ext, shards)
+    convolved, _, part = convolve(signal, gate, skip, filter_spectrum, shards)
     result = finish(convolved, part, signal, gate, skip)
     return result.reshape(positions, channels)
 

time: 387 us -> 384 us (level)
  no operation moved by 1% of the time
where the time goes in v4:
time: 384 us; the launch traced here: 381 us
  Pallas kernels  381 us (99%)
    pallas_call x1, Pallas kernels, convolve(): pl.pallas_call(kernel, out_shape=(jax.ShapeDtypeStruct((shards, ch_loc, a...  373 us
    pallas_call x1, Pallas kernels, finish(): pl.pallas_call(kernel, out_shape=jax.ShapeDtypeStruct(signal.shape, jnp.b...  7.94 us

profile of v4, /device:TPU:11, one launch (start us, length us, event | category | flops | bytes accessed | tf_op | source)
XLA Modules:
  0.0 381.2 jit_solution(6296023425397850547)
XLA Ops:
  0.0 373.3 %convolve.1 = (bf16[16,8,64,512]{3,2,1,0:T(8,128)(2,1)}, bf16[64,2,32,1024]{3,2,1,0:T(8,128)(2,1)}, bf16[48,512,128]{2,1,0:T(8,128)(2,1)}) custom-call(bf16[64,512,128]{2,1,0:T(8,128)(2,1)} %bitcast.4, bf16[64,512,128]{2,1,0:T(8,128)(2,1)} %bitcast.6, f32[1,128]{1,0:T(1,128)} %bitcast.8, bf16[2,32,1024,128]{3,2,1,0:T(8,128)(2,1)} %filt_ref.1), custom_call_target="tpu_custom_call" | custom-call | tf_op jit(solution)/shard_map/convolve/pallas_call | solution.py:546
  373.3 7.9 %finish.1 = bf16[64,512,128]{2,1,0:T(8,128)(2,1)} custom-call(bf16[16,8,64,512]{3,2,1,0:T(8,128)(2,1)} %get-tuple-element.7.conv_ref, bf16[48,512,128]{2,1,0:T(8,128)(2,1)} %get-tuple-element.8.part_ref, bf16[64,512,128]{2,1,0:T(8,128)(2,1)} %bitcast.5, bf16[64,512,128]{2,1,0:T(8,128)(2,1)} %bitcast.7, f32[1,128]{1,0:T(1,128)} %bitcast.9), custom_call_target="tpu_custom_call" | custom-call | tf_op jit(solution)/shard_map/finish/pallas_call | solution.py:669
